TPU v7x, 128 devices: a whole 4x4x4 slice. The times are simulated.
128 devices in a mesh: grid: 8 (over x, y_lo), row: 8 (over z, core), rhs: 2 (over y_hi).
Axes of the slice: x: 4, y: 4 (y_hi: 2, y_lo: 2; y = y_hi * 2 + y_lo), z: 4, core: 2. Of those that a mesh axis runs over, the one named last changes fastest.
Arguments:
- leaf_rhs: float32 [49152, 2048], P(('grid', 'row'), 'rhs'), parts along dimension 1, may hold values from -6 to 6
- block_sizes: int32 [64], P(('grid', 'row')), may hold values from 384 to 768, as said below
- leaf_lower: float32 [49152, 256], P(('grid', 'row')), may hold values from -0.25 to 0.25
- leaf_inverse: float32 [49152, 768], P(('grid', 'row')), as said below
- coupling: float32 [32768, 768], P(('grid', 'row')), may hold values from -0.02734375 to 0.02734375
- anc_rows: int32 [32768], P(('grid', 'row')), may hold values from 0 to 767, as said below
- anc_rhs: float32 [768, 2048], P(None, 'rhs'), parts along dimension 1, may hold values from -6 to 6
- anc_inverse: float32 [768, 768], replicated, as said below
Outputs:
- leaf_solution: float32 [49152, 2048], P(('grid', 'row'), 'rhs'), parts along dimension 1
- anc_solution: float32 [768, 2048], P('row', 'rhs'), parts along dimension 1
There are 2 independent parts, one for each index of `rhs`. A program takes and returns all parts, laid end to end along the dimension named above; an argument that names none is the same for every part. Nothing has to cross between parts.
Inputs may be any that keep to these rules, and one draw needn't show every extreme that they name: `block_sizes`: every value lies between 384 and 768; some block row uses all 768 rows and another exactly 384. `anc_rows`: within each block row's 512 entries the ancestor rows are distinct and increasing. `leaf_inverse`: each 768 x 768 block is lower triangular with a unit diagonal. `anc_inverse`: lower triangular with a unit diagonal.
All inputs are finite; a program needn't handle non-finite values.
Results may differ from a plain program's by a relative error of at most 0.0001.
Values sent between devices are 32-bit elements; how exact they have to be, the bound alone decides.
No kernel may reach another device: no remote copies, remote signals or barrier semaphores. Data moves between devices by JAX's collectives and lax.ppermute only.
A program may use at most 128 MiB of HBM per device.

v0:
```python
import jax
import jax.numpy as jnp
from jax import lax
from jax.experimental import pallas as pl
from jax.experimental.pallas import tpu as pltpu
from jax.sharding import Mesh
from jax.sharding import PartitionSpec as P

F32 = jnp.float32
BF16 = jnp.bfloat16
GRID_ROW = ("x", "yl", "z", "core")


def shifted(array, axis, by, sources=None):
    devices = lax.axis_size(axis)
    pairs = [(i, (i + by) % devices) for i in range(devices)]
    if sources is not None:
        pairs = [pair for pair in pairs if pair[0] in sources]
    return lax.ppermute(array, axis, pairs)


def exchanged(blocks, axes):
    return lax.all_to_all(blocks, axes, 0, 0, tiled=True)


def halves(a):
    high = a.astype(BF16)
    return high, (a - high.astype(F32)).astype(BF16)


def mxu(a, b):
    return jnp.dot(a, b, preferred_element_type=F32)


def dot3(a, b):
    return mxu(a[0], b[0]) + (mxu(a[0], b[1]) + mxu(a[1], b[0]))


def flops(m, k, n):
    return 6 * m * k * n


def cost(n_flops, n_bytes):
    return pl.CostEstimate(flops=n_flops, transcendentals=0, bytes_accessed=n_bytes)


SMEM = pl.BlockSpec(memory_space=pltpu.SMEM)
VMEM = pl.BlockSpec(memory_space=pltpu.VMEM)
LIMIT = pltpu.CompilerParams(vmem_limit_bytes=20 << 20)


def near(array):
    return pltpu.with_memory_space_constraint(array, pltpu.VMEM)


def far(array):
    return pltpu.with_memory_space_constraint(array, pltpu.HBM)


def whole(shape):
    return pl.BlockSpec(shape, lambda j: (0,) * len(shape), pipeline_mode=pl.Buffered(1))


def small(kernel, place, arrays, out, n_flops=1 << 20):
    return pl.pallas_call(
        kernel,
        grid=(1,),
        in_specs=[SMEM] + [VMEM] * len(arrays),
        out_specs=VMEM,
        out_shape=out,
        cost_estimate=cost(n_flops, 1 << 20),
        compiler_params=LIMIT,
    )(place, *arrays)


def lead_kernel(place, size, inverse, lower, rhs, a_out, b_out, send):
    rows = lax.broadcasted_iota(jnp.int32, inverse.shape, 0)
    s = halves(jnp.where(rows < size[0], inverse[...], 0.0))
    lead, half = inverse.shape[1], rhs.shape[1] // 2
    a = dot3(s, halves(lower[...]))
    a_out[...] = a
    send[:, :lead] = a
    first = dot3(s, halves(rhs[:, :half]))
    second = dot3(s, halves(rhs[:, half:]))
    own_first = place[1] == 0
    b_out[...] = jnp.where(own_first, first, second)
    send[:, lead:] = jnp.where(own_first, second, first)


def merge_kernel(place, a_own, b_own, other, out):
    low = place[1] == 0
    lead = a_own.shape[1]
    a_low = jnp.where(low, a_own[...], other[:, :lead])
    a_high = halves(jnp.where(low, other[:, :lead], a_own[...]))
    b_low = jnp.where(low, b_own[...], other[:, lead:])
    b_high = jnp.where(low, other[:, lead:], b_own[...])
    planes, tall, wide = out.shape
    half, width = tall // 2, wide // 2
    rows = tuple(jnp.where(low, part[:half], part[half:]) for part in a_high)
    mat = dot3(rows, halves(a_low))
    merged = b_high - dot3(a_high, halves(b_low))
    for i in range(planes):
        out[i, :, :width] = merged[:, i * width : (i + 1) * width]
        out[i, :half, width:] = mat[:, :width]
        out[i, half:, width:] = mat[:, width:]


def pick_kernel(place, blocks, out):
    width = out.shape[2]
    for i in range(out.shape[0]):
        out[i] = blocks[i + 1, :, width:]


def solve_kernel(place, blocks, m_own, m_other, out):
    low = place[1] == 0
    planes, _, width = out.shape
    half = m_own.shape[1] // 2
    out[0] = jnp.zeros(out.shape[1:], F32)
    carried = blocks[0, :, :width]
    out[1] = carried
    for i in range(1, planes - 1):
        right = halves(carried)
        for part in range(2):
            mine = low if part == 0 else jnp.logical_not(low)
            mat = jnp.where(mine, m_own[i - 1], m_other[i - 1])
            rows = slice(part * half, (part + 1) * half)
            moved = dot3(halves(mat[:half]), tuple(r[:width] for r in right))
            moved += dot3(halves(mat[half:]), tuple(r[width:] for r in right))
            out[i + 1, rows] = blocks[i, rows, :width] + moved
        carried = out[i + 1]


def weigh_kernel(rows, inverse, coupling, m_high, m_low, hot):
    anc, touched = hot.shape
    at = lax.broadcasted_iota(jnp.int32, (anc, touched), 0)
    hot[...] = jnp.where(at == rows[...], 1.0, 0.0).astype(BF16)
    right = halves(coupling[...])
    block = anc // 3
    for i in range(3):
        span = slice(i * block, (i + 1) * block)
        reach, cols = (i + 1) * block, min(touched, (i + 1) * block)
        high, low = halves(inverse[span, :reach])
        picked = hot[:reach, :cols]
        g = halves(mxu(high, picked) + mxu(low, picked))
        m = dot3(g, tuple(part[:cols] for part in right))
        m_high[span], m_low[span] = halves(m)


def columns_of(step, width):
    return pl.ds(pl.multiple_of(step * width, width), width)


def leaf_kernel(
    place, size, inverse, lower, rhs, b_first, other, out, sh, sl, lh, ll, t
):
    step, last = pl.program_id(0), pl.num_programs(0) - 1
    high_core = place[1] == 1
    width = t.shape[1]

    @pl.when(step == 0)
    def _():
        rows = lax.broadcasted_iota(jnp.int32, inverse.shape, 0)
        sh[...], sl[...] = halves(jnp.where(rows < size[0], inverse[...], 0.0))
        lh[...], ll[...] = halves(lower[...])

    @pl.when(step < last)
    def _():
        at = lax.rem(step, last // 2)
        second = other[:, columns_of(at + 1, width)]
        entering = jnp.where(step < last // 2, b_first[:, columns_of(at, width)], second)
        entering = jnp.where(high_core, entering, 0.0)
        t[...] = rhs[...] - dot3((lh[...], ll[...]), halves(entering))

    @pl.when(step == last)
    def _():
        t[...] = jnp.where(
            high_core, -dot3((lh[...], ll[...]), halves(other[:, :width])), lower[...]
        )

    right = halves(t[...])
    block = inverse.shape[0] // 3
    for i in range(3):
        span, reach = slice(i * block, (i + 1) * block), (i + 1) * block
        out[span] = dot3(
            (sh[span, :reach], sl[span, :reach]), (right[0][:reach], right[1][:reach])
        )


def couple_kernel(place, m_high, m_low, leaf, keep, send):
    low = place[1] == 0
    groups, planes, share, width = keep.shape
    value = dot3((m_high[...], m_low[...]), halves(leaf[...]))
    for g in range(groups):
        cols = slice(g * width, (g + 1) * width)
        for p in range(planes):
            top = value[2 * p * share : (2 * p + 1) * share, cols]
            bottom = value[(2 * p + 1) * share : (2 * p + 2) * share, cols]
            keep[g, p] = jnp.where(low, top, bottom)
            send[g, p] = jnp.where(low, bottom, top)


def entering_chip(place, own, other, step, width):
    planes, _, quarter = own.shape
    per = width // quarter
    half = planes // per
    first = lax.rem(step, half) * per
    mine = step // half == place[1]
    parts = [jnp.where(mine, own[first + i], other[first + i]) for i in range(per)]
    return halves(jnp.concatenate(parts, axis=1))


def update_kernel(place, own, other, n_keep, n_arrived, keep, arrived, out, nh, nl):
    groups, planes, share, width = out.shape
    tall = planes * share

    @pl.when(pl.program_id(0) == 0)
    def _():
        for g in range(groups):
            cols = slice(g * width, (g + 1) * width)
            n = (n_keep[g] + n_arrived[g]).reshape(tall, width)
            nh[:, cols], nl[:, cols] = halves(n)

    carried = entering_chip(place, own, other, pl.program_id(0), groups * width)
    moved = dot3((nh[...], nl[...]), carried)
    for g in range(groups):
        c = (keep[g] + arrived[g]).reshape(tall, width)
        out[g] = (c - moved[:, g * width : (g + 1) * width]).reshape(planes, share, width)


def finish_kernel(place, own, other, h, f, sol, hh, hl):
    step = pl.program_id(0)

    @pl.when(step == 0)
    def _():
        hh[...], hl[...] = halves(h[...])

    carried = entering_chip(place, own, other, step, sol.shape[1])
    sol[...] = f[...] - dot3((hh[...], hl[...]), carried)


def total_kernel(own_rows, own_cols, arrived, out):
    total = arrived[0]
    for i in range(1, arrived.shape[0]):
        total = total + arrived[i]
    block = dot3(halves(own_rows[...]), halves(own_cols[...])) - total
    for g in range(out.shape[0]):
        out[g] = block


def whole_body(leaf_rhs, block_sizes, leaf_lower, leaf_inverse, coupling, anc_rows, anc_rhs, anc_inverse):
    rows, columns = leaf_rhs.shape
    lead = leaf_lower.shape[1]
    anc, touched = anc_inverse.shape[0], anc_rows.shape[0]
    planes, cores = lax.axis_size("z"), lax.axis_size("core")
    groups = lax.axis_size("x") * lax.axis_size("yl")
    z, core = lax.axis_index("z"), lax.axis_index("core")
    place = jnp.stack([z, core]).astype(jnp.int32)
    half, quarter = columns // cores, columns // (cores * planes)
    share, width = anc // (planes * cores), columns // groups

    block = lambda r, c: whole((r, c))
    a_own, b_own, send = pl.pallas_call(
        lead_kernel,
        grid=(1,),
        in_specs=[SMEM, SMEM, block(lead, lead), block(lead, lead), block(lead, columns)],
        out_specs=[VMEM] * 3,
        out_shape=[pltpu.VMEM((lead, w), F32) for w in (lead, half, lead + half)],
        cost_estimate=cost(flops(lead, lead, lead + columns), 1 << 21),
        compiler_params=LIMIT,
        name="lead",
    )(place, block_sizes, far(leaf_inverse), far(leaf_lower), far(leaf_rhs))
    other = shifted(send, "core", 1)
    blocks = small(
        merge_kernel,
        place,
        (near(a_own), near(b_own), near(other)),
        pltpu.HBM((planes, lead, 2 * quarter), F32),
        flops(lead, lead, half + lead // cores),
    )
    blocks = exchanged(blocks, "z")
    b_low = shifted(b_own, "core", 1, (0,))
    mat_shape = (planes - 2, lead, lead // cores)
    mats_own = small(pick_kernel, place, (far(blocks),), pltpu.VMEM(mat_shape, F32))
    mats_other = shifted(mats_own, "core", 1)

    m_high, m_low = pl.pallas_call(
        weigh_kernel,
        out_shape=[pltpu.HBM((anc, rows), BF16)] * 2,
        scratch_shapes=[pltpu.VMEM((anc, touched), BF16)],
        cost_estimate=cost(flops(anc, touched, rows + anc), 1 << 22),
        compiler_params=LIMIT,
        name="weigh",
    )(anc_rows[None], far(anc_inverse), far(coupling))

    step = 2 * width
    steps = columns // step
    tall = pl.BlockSpec((rows, step), lambda j: (0, j))
    blocked = pl.BlockSpec((step // width, planes, share, width), lambda j: (j, 0, 0, 0))
    last = pl.BlockSpec((step // width, planes, share, width), lambda j: (steps, 0, 0, 0))
    leaf = pl.pallas_call(
        leaf_kernel,
        grid=(steps + 1,),
        in_specs=[
            SMEM,
            SMEM,
            whole((rows, rows)),
            whole((rows, lead)),
            pl.BlockSpec((rows, step), lambda j: (0, jnp.minimum(j, steps - 1))),
            whole(b_low.shape),
            whole(other.shape),
        ],
        out_specs=tall,
        out_shape=pltpu.HBM((rows, columns + lead), F32),
        scratch_shapes=[pltpu.VMEM((rows, rows), BF16)] * 2
        + [pltpu.VMEM((rows, lead), BF16)] * 2
        + [pltpu.VMEM((rows, step), F32)],
        cost_estimate=cost(flops(rows, rows, columns), 1 << 23),
        compiler_params=LIMIT,
        name="leaf",
    )(
        place,
        block_sizes,
        far(leaf_inverse),
        far(leaf_lower),
        far(leaf_rhs),
        far(b_low),
        far(other),
    )

    ends = small(
        solve_kernel,
        place,
        (far(blocks), near(mats_own), near(mats_other)),
        pltpu.HBM((planes, lead, quarter), F32),
        flops(lead, lead, 2 * quarter),
    )
    own = exchanged(ends, "z")
    own_other = shifted(own, "core", 1)
    wide = (columns + lead) // width
    keep, send = pl.pallas_call(
        couple_kernel,
        grid=(steps + 1,),
        in_specs=[SMEM, whole((anc, rows)), whole((anc, rows)), tall],
        out_specs=[blocked] * 2,
        out_shape=[pltpu.HBM((wide, planes, share, width), F32)] * 2,
        cost_estimate=cost(flops(anc, rows, columns + lead), 1 << 23),
        compiler_params=LIMIT,
        name="couple",
    )(place, far(m_high), far(m_low), far(leaf))
    keep_other = shifted(send, "core", 1)
    ends_spec = whole((planes, lead, quarter))
    update = pl.pallas_call(
        update_kernel,
        grid=(steps,),
        in_specs=[SMEM, ends_spec, ends_spec, last, last, blocked, blocked],
        out_specs=blocked,
        out_shape=pltpu.HBM((groups, planes, share, width), F32),
        scratch_shapes=[pltpu.VMEM((planes * share, lead), BF16)] * 2,
        cost_estimate=cost(flops(planes * share, lead, columns), 1 << 22),
        compiler_params=LIMIT,
        name="update",
    )(place, far(own), near(own_other), *[far(a) for a in (keep, keep_other)] * 2)
    update = update.reshape(groups * planes, share, width)
    arrived = exchanged(update, ("x", "yl", "z"))
    sol = pl.pallas_call(
        finish_kernel,
        grid=(steps,),
        in_specs=[SMEM, ends_spec, ends_spec, pl.BlockSpec((rows, step), lambda j: (0, steps)), tall],
        out_specs=tall,
        out_shape=jax.ShapeDtypeStruct((rows, columns), F32),
        scratch_shapes=[pltpu.VMEM((rows, lead), BF16)] * 2,
        cost_estimate=cost(flops(rows, lead, columns), 1 << 23),
        compiler_params=LIMIT,
        name="finish",
    )(place, far(own), far(own_other), far(leaf), far(leaf))

    group = lax.axis_index(("x", "yl"))
    own_rows = lax.dynamic_slice_in_dim(anc_inverse, (z * cores + core) * share, share, 0)
    own_cols = lax.dynamic_slice_in_dim(anc_rhs, group * width, width, 1)
    anc_blocks = pl.pallas_call(
        total_kernel,
        in_specs=[VMEM] * 3,
        out_specs=VMEM,
        out_shape=pltpu.VMEM((groups, share, width), F32),
        cost_estimate=cost(flops(share, anc, width), 1 << 21),
        compiler_params=LIMIT,
        name="total",
    )(own_rows, own_cols, near(arrived))
    spread = exchanged(anc_blocks, ("x", "yl"))
    return sol, jnp.moveaxis(spread, 0, 1).reshape(share, columns)


def solution(mesh):
    split = Mesh(
        mesh.devices.reshape(4, 2, 4, 2, mesh.shape["rhs"]), ("x", "yl", "z", "core", "rhs")
    )
    in_specs = (
        P(GRID_ROW, "rhs"),
        P(GRID_ROW),
        P(GRID_ROW, None),
        P(GRID_ROW, None),
        P(GRID_ROW, None),
        P(GRID_ROW),
        P(None, "rhs"),
        P(),
    )
    out_specs = (P(GRID_ROW, "rhs"), P(("z", "core"), "rhs"))
    return jax.shard_map(whole_body, mesh=split, in_specs=in_specs, out_specs=out_specs, check_vma=False)
```

profile of v0, /device:TPU:0, one launch (start us, length us, event | category | flops | bytes accessed | tf_op | source)
XLA Modules:
  0.0 117.2 jit_solution(3306220820841338784)
XLA Ops:
  0.6 0.0 copy-start
  1.4 0.1 pad_add_fusion.place
  1.5 3.0 %lead.1 = (f32[256,256]{1,0:T(8,128)S(1)}, f32[256,512]{1,0:T(8,128)}, f32[256,768]{1,0:T(8,128)S(1)}) custom-call(s32[2]{0:T(128)S(1)} %pad_add_fusion.place, s32[1]{0:T(128)S(6)} %copy.13.size, f32[768,768]{1,0:T(8,128)} %inverse.4, f32[768,256]{1,0:T(8,128)} %lower.3, f32[768,1024]{1,0:T(8,128)} %rhs.3), custom_call_target="tpu_custom_call" | custom-call | flops 503316480 | bytes 2097152 | tf_op jit(solution)/shard_map/lead/pallas_call | solution.py:262
  4.5 0.0 collective-permute-start
  4.5 3.2 %collective-permute-start.3 = (f32[256,512]{1,0:T(8,128)}, f32[256,512]{1,0:T(8,128)}, u32[]{:S(2)}, u32[]{:S(2)}) collective-permute-start(f32[256,512]{1,0:T(8,128)} %get-tuple-element.10.b_own), channel_id=1, source_target_pairs={{0,2},{1,3},{4,6},{5,7},{8,10},{9,11},{12,14},{13,15},{16,18},{17,... | collective-permute-start | bytes 1572872 | tf_op jit(solution)/shard_map/ppermute | solution.py:19
  7.7 7.3 %weigh.1 = (bf16[768,768]{1,0:T(8,128)(2,1)}, bf16[768,768]{1,0:T(8,128)(2,1)}) custom-call(s32[1,512]{1,0:T(1,128)S(1)} %bitcast.10, f32[768,768]{1,0:T(8,128)} %inverse.5, f32[512,768]{1,0:T(8,128)} %coupling.1), custom_call_target="tpu_custom_call" | custom-call | flops 3623878656 | bytes 4194304 | tf_op jit(solution)/shard_map/weigh/pallas_call | solution.py:286
  15.0 2.5 %shard_map.95 = f32[4,256,256]{2,1,0:T(8,128)} custom-call(s32[2]{0:T(128)S(1)} %pad_add_fusion.place, f32[256,256]{1,0:T(8,128)S(1)} %get-tuple-element.9.a_own, f32[256,512]{1,0:T(8,128)} %get-tuple-element.10.b_own, f32[256,768]{1,0:T(8,128)S(1)} %collective-permute-done.other), custom_call_target="tpu_custom_call" | custom-call | flops 251658240 | bytes 1048576 | tf_op jit(solution)/shard_map/pallas_call | solution.py:65
  17.6 0.9 copy-done.3
  18.5 5.4 %all-to-all-start = ((f32[4,256,256]{2,1,0:T(8,128)}), f32[4,256,256]{2,1,0:T(8,128)}, u32[]{:S(2)}, u32[]{:S(2)}) async-start(f32[4,256,256]{2,1,0:T(8,128)} %shard_map.95), calls=%async_computation | async-start | bytes 2097152 | tf_op jit(solution)/shard_map/all_to_all | solution.py:23
  23.9 10.6 %leaf.1.h.f = f32[768,1280]{1,0:T(8,128)} custom-call(s32[2]{0:T(128)S(1)} %pad_add_fusion.place, s32[1]{0:T(128)S(6)} %copy.13.size, f32[768,768]{1,0:T(8,128)} %inverse.4, f32[768,256]{1,0:T(8,128)} %lower.3, f32[768,1024]{1,0:T(8,128)} %rhs.3, f32[256,512]{1,0:T(8,128)} %collective-permute-done.3.b_first, f32[256,768]{1,0:T(8,128)} %copy-done.3), custom_call_target="tpu_custom_call" | custom-call | flops 3623878656 | bytes 8388608 | tf_op jit(solution)/shard_map/leaf/pallas_call | solution.py:300
  34.5 9.0 %couple.1 = (f32[10,4,96,128]{3,2,1,0:T(8,128)}, f32[10,4,96,128]{3,2,1,0:T(8,128)}) custom-call(s32[2]{0:T(128)S(1)} %pad_add_fusion.place, bf16[768,768]{1,0:T(8,128)(2,1)} %get-tuple-element.12.m_high, bf16[768,768]{1,0:T(8,128)(2,1)} %get-tuple-element.13.m_low, f32[768,1280]{1,0:T(8,128)} %leaf.1.h.f), custom_call_target="tpu_custom_call" | custom-call | flops 4529848320 | bytes 8388608 | tf_op jit(solution)/shard_map/couple/pallas_call | solution.py:340
  43.4 0.0 collective-permute-start.4
  43.4 0.0 all-to-all-done.blocks
  43.4 1.3 %shard_map.96.m_own = f32[2,256,128]{2,1,0:T(8,128)S(1)} custom-call(s32[2]{0:T(128)S(1)} %pad_add_fusion.place, f32[4,256,256]{2,1,0:T(8,128)} %all-to-all-done.blocks), custom_call_target="tpu_custom_call" | custom-call | flops 1048576 | bytes 1048576 | tf_op jit(solution)/shard_map/pallas_call | solution.py:65
  44.7 0.6 collective-permute-start.1
  45.3 2.7 %collective-permute-done.1.m_other = f32[2,256,128]{2,1,0:T(8,128)S(1)} collective-permute-done((f32[2,256,128]{2,1,0:T(8,128)S(1)}, f32[2,256,128]{2,1,0:T(8,128)S(1)}, u32[]{:S(2)}, u32[]{:S(2)}) %collective-permute-start.1) | collective-permute-done | bytes 262176 | tf_op jit(solution)/shard_map/ppermute | solution.py:19
  48.0 2.6 %shard_map.97 = f32[4,256,128]{2,1,0:T(8,128)} custom-call(s32[2]{0:T(128)S(1)} %pad_add_fusion.place, f32[4,256,256]{2,1,0:T(8,128)} %all-to-all-done.blocks, f32[2,256,128]{2,1,0:T(8,128)S(1)} %shard_map.96.m_own, f32[2,256,128]{2,1,0:T(8,128)S(1)} %collective-permute-done.1.m_other), custom_call_target="tpu_custom_call" | custom-call | flops 100663296 | bytes 1048576 | tf_op jit(solution)/shard_map/pallas_call | solution.py:65
  50.5 14.6 %all_to_all.20.own = f32[4,256,128]{2,1,0:T(8,128)S(1)} all-to-all(f32[4,256,128]{2,1,0:T(8,128)} %shard_map.97), channel_id=1, replica_groups=mesh['x'=4,'yl'=2,'z'=4,'core'=2,'rhs'=2] {'z'}, dimensions={0} | all-to-all | bytes 1048576 | tf_op jit(solution)/shard_map/all_to_all | solution.py:23
  65.1 0.0 collective-permute-start.2
  65.1 1.9 %collective-permute-done.2.other = f32[4,256,128]{2,1,0:T(8,128)S(1)} collective-permute-done((f32[4,256,128]{2,1,0:T(8,128)S(1)}, f32[4,256,128]{2,1,0:T(8,128)S(1)}, u32[]{:S(2)}, u32[]{:S(2)}) %collective-permute-start.2) | collective-permute-done | bytes 524320 | tf_op jit(solution)/shard_map/ppermute | solution.py:19
  67.0 0.0 collective-permute-done.4.n_arrived.arrived
  67.0 5.2 %update.1 = f32[8,4,96,128]{3,2,1,0:T(8,128)} custom-call(s32[2]{0:T(128)S(1)} %pad_add_fusion.place, f32[4,256,128]{2,1,0:T(8,128)} %copy-done.5, f32[4,256,128]{2,1,0:T(8,128)S(1)} %collective-permute-done.2.other, f32[10,4,96,128]{3,2,1,0:T(8,128)} %get-tuple-element.14.n_keep.keep, f32[10,4,96,128]{3,2,1,0:T(8,128)} %collective-permute-done.4.n_arrived.arrived, ...), custom_call_target="tpu_custom_call" | custom-call | flops 603979776 | bytes 4194304 | tf_op jit(solution)/shard_map/update/pallas_call | solution.py:352
  72.2 6.4 %all-to-all-start.2 = ((f32[32,96,128]{2,1,0:T(8,128)}), f32[32,96,128]{2,1,0:T(8,128)}, u32[]{:S(2)}, u32[]{:S(2)}) async-start(f32[32,96,128]{2,1,0:T(8,128)} %bitcast.11), calls=%async_computation.2 | async-start | bytes 3145728 | tf_op jit(solution)/shard_map/all_to_all | solution.py:23
  78.6 1.7 %constant_dynamic-slice_fusion.1.own_rows = f32[96,768]{1,0:T(8,128)} fusion(f32[768,768]{1,0:T(8,128)} %inverse.5, s32[]{:T(128)S(6)} %select_n.6), kind=kLoop, calls=%fused_computation.3 | loop fusion | bytes 589828 | tf_op jit(solution)/shard_map/dynamic_slice | solution.py:378
  80.4 0.1 constant_dynamic-slice_fusion.own_cols
  80.4 20.7 %all-to-all-done.2.arrived = f32[32,96,128]{2,1,0:T(8,128)} async-done(((f32[32,96,128]{2,1,0:T(8,128)}), f32[32,96,128]{2,1,0:T(8,128)}, u32[]{:S(2)}, u32[]{:S(2)}) %all-to-all-start.2) | async-done | bytes 1572896 | tf_op jit(solution)/shard_map/all_to_all | solution.py:23
  101.1 1.0 copy-done.2
  102.1 2.5 %total.1 = f32[8,96,128]{2,1,0:T(8,128)} custom-call(f32[96,768]{1,0:T(8,128)S(1)} %copy-done.2, f32[768,128]{1,0:T(8,128)S(1)} %constant_dynamic-slice_fusion.own_cols, f32[32,96,128]{2,1,0:T(8,128)} %all-to-all-done.2.arrived), custom_call_target="tpu_custom_call" | custom-call | flops 56623104 | bytes 2097152 | tf_op jit(solution)/shard_map/total/pallas_call | solution.py:380
  104.6 3.8 %all-to-all-start.3 = ((f32[8,96,128]{2,1,0:T(8,128)}), f32[8,96,128]{2,1,0:T(8,128)S(1)}, u32[]{:S(2)}, u32[]{:S(2)}) async-start(f32[8,96,128]{2,1,0:T(8,128)} %total.1), calls=%async_computation.3 | async-start | bytes 786432 | tf_op jit(solution)/shard_map/all_to_all | solution.py:23
  108.4 5.8 %finish.1 = f32[768,1024]{1,0:T(8,128)} custom-call(s32[2]{0:T(128)S(1)} %pad_add_fusion.place, f32[4,256,128]{2,1,0:T(8,128)} %copy-done.5, f32[4,256,128]{2,1,0:T(8,128)} %copy-done.1, f32[768,1280]{1,0:T(8,128)} %leaf.1.h.f, f32[768,1280]{1,0:T(8,128)} %leaf.1.h.f), custom_call_target="tpu_custom_call" | custom-call | flops 1207959552 | bytes 8388608 | tf_op jit(solution)/shard_map/finish/pallas_call | solution.py:365
  114.2 2.2 %all-to-all-done.3 = f32[8,96,128]{2,1,0:T(8,128)S(1)} async-done(((f32[8,96,128]{2,1,0:T(8,128)}), f32[8,96,128]{2,1,0:T(8,128)S(1)}, u32[]{:S(2)}, u32[]{:S(2)}) %all-to-all-start.3) | async-done | bytes 393248 | tf_op jit(solution)/shard_map/all_to_all | solution.py:23
  116.4 0.8 copy_bitcast_fusion
  (11 shorter events, 0.0 us)
Async XLA Ops:
  0.6 79.7 %copy-start = (f32[768,1024]{1,0:T(8,128)S(1)}, f32[768,1024]{1,0:T(8,128)}, u32[]{:S(2)}) copy-start(f32[768,1024]{1,0:T(8,128)} %param.14) | copy-start | bytes 9437188
  1.5 6.2 %copy-start.4 = (s32[512]{0:T(512)S(1)}, s32[512]{0:T(512)}, u32[]{:S(2)}) copy-start(s32[512]{0:T(512)} %param.13) | copy-start | bytes 6148
  4.5 10.5 %collective-permute-start = (f32[256,768]{1,0:T(8,128)S(1)}, f32[256,768]{1,0:T(8,128)S(1)}, u32[]{:S(2)}, u32[]{:S(2)}) collective-permute-start(f32[256,768]{1,0:T(8,128)S(1)} %get-tuple-element.11), channel_id=1, source_target_pairs={{0,2},{2,0},{1,3},{3,1},{4,6},{6,4},{5,7},{7,5},{8,10},{10,8},{9,1... | collective-permute-start | bytes 2359304 | tf_op jit(solution)/shard_map/ppermute | solution.py:19
  4.5 19.4 %collective-permute-start.3 = (f32[256,512]{1,0:T(8,128)}, f32[256,512]{1,0:T(8,128)}, u32[]{:S(2)}, u32[]{:S(2)}) collective-permute-start(f32[256,512]{1,0:T(8,128)} %get-tuple-element.10.b_own), channel_id=1, source_target_pairs={{0,2},{1,3},{4,6},{5,7},{8,10},{9,11},{12,14},{13,15},{16,18},{17,... | collective-permute-start | bytes 1572872 | tf_op jit(solution)/shard_map/ppermute | solution.py:19
  17.6 0.9 copy-start.3
  18.5 24.9 %all-to-all-start = ((f32[4,256,256]{2,1,0:T(8,128)}), f32[4,256,256]{2,1,0:T(8,128)}, u32[]{:S(2)}, u32[]{:S(2)}) async-start(f32[4,256,256]{2,1,0:T(8,128)} %shard_map.95), calls=%async_computation | async-start | bytes 2097152 | tf_op jit(solution)/shard_map/all_to_all | solution.py:23
  43.4 23.6 %collective-permute-start.4 = (f32[10,4,96,128]{3,2,1,0:T(8,128)}, f32[10,4,96,128]{3,2,1,0:T(8,128)}, u32[]{:S(2)}, u32[]{:S(2)}) collective-permute-start(f32[10,4,96,128]{3,2,1,0:T(8,128)} %get-tuple-element.15), channel_id=1, source_target_pairs={{0,2},{2,0},{1,3},{3,1},{4,6},{6,4},{5,7},{7,5},{8,10},{10,8},{9,1... | collective-permute-start | bytes 5898248 | tf_op jit(solution)/shard_map/ppermute | solution.py:19
  44.7 3.3 %collective-permute-start.1 = (f32[2,256,128]{2,1,0:T(8,128)S(1)}, f32[2,256,128]{2,1,0:T(8,128)S(1)}, u32[]{:S(2)}, u32[]{:S(2)}) collective-permute-start(f32[2,256,128]{2,1,0:T(8,128)S(1)} %shard_map.96.m_own), channel_id=1, source_target_pairs={{0,2},{2,0},{1,3},{3,1},{4,6},{6,4},{5,7},{7,5},{8,10},{10,8},{9,1... | collective-permute-start | bytes 786440 | tf_op jit(solution)/shard_map/ppermute | solution.py:19
  65.1 1.9 %copy-start.5 = (f32[4,256,128]{2,1,0:T(8,128)}, f32[4,256,128]{2,1,0:T(8,128)S(1)}, u32[]{:S(2)}) copy-start(f32[4,256,128]{2,1,0:T(8,128)S(1)} %all_to_all.20.own) | copy-start | bytes 1572868
  65.1 1.9 %collective-permute-start.2 = (f32[4,256,128]{2,1,0:T(8,128)S(1)}, f32[4,256,128]{2,1,0:T(8,128)S(1)}, u32[]{:S(2)}, u32[]{:S(2)}) collective-permute-start(f32[4,256,128]{2,1,0:T(8,128)S(1)} %all_to_all.20.own), channel_id=1, source_target_pairs={{0,2},{2,0},{1,3},{3,1},{4,6},{6,4},{5,7},{7,5},{8,10},{10,8},{9,1... | collective-permute-start | bytes 1572872 | tf_op jit(solution)/shard_map/ppermute | solution.py:19
  67.0 5.2 %copy-start.1 = (f32[4,256,128]{2,1,0:T(8,128)}, f32[4,256,128]{2,1,0:T(8,128)S(1)}, u32[]{:S(2)}) copy-start(f32[4,256,128]{2,1,0:T(8,128)S(1)} %collective-permute-done.2.other) | copy-start | bytes 1572868
  72.2 28.9 %all-to-all-start.2 = ((f32[32,96,128]{2,1,0:T(8,128)}), f32[32,96,128]{2,1,0:T(8,128)}, u32[]{:S(2)}, u32[]{:S(2)}) async-start(f32[32,96,128]{2,1,0:T(8,128)} %bitcast.11), calls=%async_computation.2 | async-start | bytes 3145728 | tf_op jit(solution)/shard_map/all_to_all | solution.py:23
  101.1 1.0 copy-start.2
  104.6 11.8 %all-to-all-start.3 = ((f32[8,96,128]{2,1,0:T(8,128)}), f32[8,96,128]{2,1,0:T(8,128)S(1)}, u32[]{:S(2)}, u32[]{:S(2)}) async-start(f32[8,96,128]{2,1,0:T(8,128)} %total.1), calls=%async_computation.3 | async-start | bytes 786432 | tf_op jit(solution)/shard_map/all_to_all | solution.py:23
where the time goes:
time: 118 us; the launch traced here: 117 us
  Pallas kernels  49.6 us (42%)
  waiting for transfers between devices  27.5 us (23%)
  starting transfers between devices  19.5 us (17%)
  blocking collectives  14.6 us (12%)
  local copies, waits for them, and re-layouts  4.39 us (4%)
  between operations  1.5 us (1%)
    all_to_all x3, waiting for transfers between devices, exchanged(): return lax.all_to_all(blocks, axes, 0, 0, tiled=True)  22.9 us
    all_to_all x3, starting transfers between devices, exchanged(): return lax.all_to_all(blocks, axes, 0, 0, tiled=True)  15.7 us
    all_to_all x1, blocking collectives, exchanged(): return lax.all_to_all(blocks, axes, 0, 0, tiled=True)  14.6 us
    pallas_call x1, Pallas kernels, whole_body(): pl.pallas_call(leaf_kernel, grid=(steps + 1,), in_specs=[SMEM, SMEM, whol...  10.6 us
    pallas_call x1, Pallas kernels, whole_body(): pl.pallas_call(couple_kernel, grid=(steps + 1,), in_specs=[SMEM, whole((a...  8.95 us
    pallas_call x1, Pallas kernels, whole_body(): pl.pallas_call(weigh_kernel, out_shape=[pltpu.HBM((anc, rows), BF16)] * 2...  7.31 us
    pallas_call x3, Pallas kernels, small(): pl.pallas_call(kernel, grid=(1,), in_specs=[SMEM] + [VMEM] * len(arrays),...  6.36 us
    pallas_call x1, Pallas kernels, whole_body(): pl.pallas_call(finish_kernel, grid=(steps,), in_specs=[SMEM, ends_spec, e...  5.79 us
  transfers between devices with their start and end apart: 8, of which 4 were waited for; matrix products, arithmetic and copies ran while one was open for 1% of the time, Pallas kernels for 33%

commit v1 on v0

--- a/solution.py
+++ b/solution.py
@@ -23,6 +23,10 @@
     return lax.all_to_all(blocks, axes, 0, 0, tiled=True)
 
 
+def swapped(blocks):
+    return [blocks[0]] + [shifted(b, "z", s) for s, b in enumerate(blocks) if s]
+
+
 def halves(a):
     high = a.astype(BF16)
     return high, (a - high.astype(F32)).astype(BF16)
@@ -61,16 +65,16 @@
     return pl.BlockSpec(shape, lambda j: (0,) * len(shape), pipeline_mode=pl.Buffered(1))
 
 
-def small(kernel, place, arrays, out, n_flops=1 << 20):
+def small(kernel, place, arrays, outs, scratch=(), n_flops=1 << 20):
     return pl.pallas_call(
         kernel,
-        grid=(1,),
         in_specs=[SMEM] + [VMEM] * len(arrays),
-        out_specs=VMEM,
-        out_shape=out,
+        out_specs=[VMEM] * len(outs),
+        out_shape=[pltpu.VMEM(shape, F32) for shape in outs],
+        scratch_shapes=list(scratch),
         cost_estimate=cost(n_flops, 1 << 20),
         compiler_params=LIMIT,
-    )(place, *arrays)
+    )(place, *[near(a) for a in arrays])
 
 
 def lead_kernel(place, size, inverse, lower, rhs, a_out, b_out, send):
@@ -87,37 +91,43 @@
     send[:, lead:] = jnp.where(own_first, second, first)
 
 
-def merge_kernel(place, a_own, b_own, other, out):
-    low = place[1] == 0
+def merge_kernel(place, a_own, b_own, other, o0, o1, o2, o3, quarters):
+    z, low = place[0], place[1] == 0
     lead = a_own.shape[1]
     a_low = jnp.where(low, a_own[...], other[:, :lead])
     a_high = halves(jnp.where(low, other[:, :lead], a_own[...]))
     b_low = jnp.where(low, b_own[...], other[:, lead:])
     b_high = jnp.where(low, other[:, lead:], b_own[...])
-    planes, tall, wide = out.shape
-    half, width = tall // 2, wide // 2
+    planes, tall, width = quarters.shape
+    half = tall // 2
     rows = tuple(jnp.where(low, part[:half], part[half:]) for part in a_high)
     mat = dot3(rows, halves(a_low))
     merged = b_high - dot3(a_high, halves(b_low))
     for i in range(planes):
-        out[i, :, :width] = merged[:, i * width : (i + 1) * width]
-        out[i, :half, width:] = mat[:, :width]
-        out[i, half:, width:] = mat[:, width:]
-
-
-def pick_kernel(place, blocks, out):
-    width = out.shape[2]
+        quarters[i] = merged[:, i * width : (i + 1) * width]
+    for s, out in enumerate((o0, o1, o2, o3)):
+        out[:, :width] = quarters[lax.rem(z + s, planes)]
+        out[:half, width:] = mat[:, :width]
+        out[half:, width:] = mat[:, width:]
+
+
+def pick_kernel(place, r0, r1, r2, r3, out, mats):
+    planes, _, width = mats.shape
+    for s, r in enumerate((r0, r1, r2, r3)):
+        mats[lax.rem(place[0] + planes - s, planes)] = r[:, width:]
     for i in range(out.shape[0]):
-        out[i] = blocks[i + 1, :, width:]
-
-
-def solve_kernel(place, blocks, m_own, m_other, out):
-    low = place[1] == 0
-    planes, _, width = out.shape
+        out[i] = mats[i + 1]
+
+
+def solve_kernel(place, r0, r1, r2, r3, m_own, m_other, o0, o1, o2, o3, blocks, ends):
+    z, low = place[0], place[1] == 0
+    planes, _, width = ends.shape
     half = m_own.shape[1] // 2
-    out[0] = jnp.zeros(out.shape[1:], F32)
-    carried = blocks[0, :, :width]
-    out[1] = carried
+    for s, r in enumerate((r0, r1, r2, r3)):
+        blocks[lax.rem(z + planes - s, planes)] = r[:, :width]
+    ends[0] = jnp.zeros(ends.shape[1:], F32)
+    carried = blocks[0]
+    ends[1] = carried
     for i in range(1, planes - 1):
         right = halves(carried)
         for part in range(2):
@@ -126,8 +136,16 @@
             rows = slice(part * half, (part + 1) * half)
             moved = dot3(halves(mat[:half]), tuple(r[:width] for r in right))
             moved += dot3(halves(mat[half:]), tuple(r[width:] for r in right))
-            out[i + 1, rows] = blocks[i, rows, :width] + moved
-        carried = out[i + 1]
+            ends[i + 1, rows] = blocks[i, rows] + moved
+        carried = ends[i + 1]
+    for s, out in enumerate((o0, o1, o2, o3)):
+        out[...] = ends[lax.rem(z + s, planes)]
+
+
+def gather_kernel(place, t0, t1, t2, t3, out):
+    planes = out.shape[0]
+    for s, t in enumerate((t0, t1, t2, t3)):
+        out[lax.rem(place[0] + planes - s, planes)] = t[...]
 
 
 def weigh_kernel(rows, inverse, coupling, m_high, m_low, hot):
@@ -179,24 +197,28 @@
 
     right = halves(t[...])
     block = inverse.shape[0] // 3
+    cols = columns_of(step, width)
     for i in range(3):
         span, reach = slice(i * block, (i + 1) * block), (i + 1) * block
-        out[span] = dot3(
+        out[span, cols] = dot3(
             (sh[span, :reach], sl[span, :reach]), (right[0][:reach], right[1][:reach])
         )
 
 
 def couple_kernel(place, m_high, m_low, leaf, keep, send):
     low = place[1] == 0
-    groups, planes, share, width = keep.shape
-    value = dot3((m_high[...], m_low[...]), halves(leaf[...]))
+    step = pl.program_id(0)
+    planes, share, width = keep.shape[1:]
+    wide = leaf.shape[1] // pl.num_programs(0)
+    value = dot3((m_high[...], m_low[...]), halves(leaf[:, columns_of(step, wide)]))
+    groups = wide // width
     for g in range(groups):
         cols = slice(g * width, (g + 1) * width)
         for p in range(planes):
             top = value[2 * p * share : (2 * p + 1) * share, cols]
             bottom = value[(2 * p + 1) * share : (2 * p + 2) * share, cols]
-            keep[g, p] = jnp.where(low, top, bottom)
-            send[g, p] = jnp.where(low, bottom, top)
+            keep[step * groups + g, p] = jnp.where(low, top, bottom)
+            send[step * groups + g, p] = jnp.where(low, bottom, top)
 
 
 def entering_chip(place, own, other, step, width):
@@ -209,42 +231,58 @@
     return halves(jnp.concatenate(parts, axis=1))
 
 
-def update_kernel(place, own, other, n_keep, n_arrived, keep, arrived, out, nh, nl):
+def update_kernel(place, own, other, keep, arrived, out, nh, nl):
     groups, planes, share, width = out.shape
-    tall = planes * share
-
-    @pl.when(pl.program_id(0) == 0)
+    tall, step, steps = planes * share, pl.program_id(0), pl.num_programs(0)
+
+    @pl.when(step == 0)
     def _():
         for g in range(groups):
             cols = slice(g * width, (g + 1) * width)
-            n = (n_keep[g] + n_arrived[g]).reshape(tall, width)
+            n = (keep[steps * groups + g] + arrived[steps * groups + g]).reshape(tall, width)
             nh[:, cols], nl[:, cols] = halves(n)
 
-    carried = entering_chip(place, own, other, pl.program_id(0), groups * width)
+    carried = entering_chip(place, own, other, step, groups * width)
     moved = dot3((nh[...], nl[...]), carried)
     for g in range(groups):
-        c = (keep[g] + arrived[g]).reshape(tall, width)
+        c = (keep[step * groups + g] + arrived[step * groups + g]).reshape(tall, width)
         out[g] = (c - moved[:, g * width : (g + 1) * width]).reshape(planes, share, width)
 
 
-def finish_kernel(place, own, other, h, f, sol, hh, hl):
+def finish_kernel(place, own, other, leaf, sol, hh, hl):
     step = pl.program_id(0)
+    width = sol.shape[1]
 
     @pl.when(step == 0)
     def _():
-        hh[...], hl[...] = halves(h[...])
-
-    carried = entering_chip(place, own, other, step, sol.shape[1])
-    sol[...] = f[...] - dot3((hh[...], hl[...]), carried)
-
-
-def total_kernel(own_rows, own_cols, arrived, out):
-    total = arrived[0]
+        hh[...], hl[...] = halves(leaf[:, pl.num_programs(0) * width :])
+
+    carried = entering_chip(place, own, other, step, width)
+    sol[...] = leaf[:, columns_of(step, width)] - dot3((hh[...], hl[...]), carried)
+
+
+def right_kernel(rows, cols, out):
+    out[...] = dot3(halves(rows[...]), halves(cols[...]))
+
+
+def total_kernel(right, arrived, out, total):
+    step = pl.program_id(0)
+    part = arrived[0]
     for i in range(1, arrived.shape[0]):
-        total = total + arrived[i]
-    block = dot3(halves(own_rows[...]), halves(own_cols[...])) - total
-    for g in range(out.shape[0]):
-        out[g] = block
+        part = part + arrived[i]
+
+    @pl.when(step == 0)
+    def _():
+        total[...] = right[...] - part
+
+    @pl.when(step > 0)
+    def _():
+        total[...] = total[...] - part
+
+    @pl.when(step == pl.num_programs(0) - 1)
+    def _():
+        for g in range(out.shape[0]):
+            out[g] = total[...]
 
 
 def whole_body(leaf_rhs, block_sizes, leaf_lower, leaf_inverse, coupling, anc_rows, anc_rhs, anc_inverse):
@@ -258,7 +296,7 @@
     half, quarter = columns // cores, columns // (cores * planes)
     share, width = anc // (planes * cores), columns // groups
 
-    block = lambda r, c: whole((r, c))
+    block = lambda r, c: pl.BlockSpec((r, c), lambda i: (0, 0))
     a_own, b_own, send = pl.pallas_call(
         lead_kernel,
         grid=(1,),
@@ -273,30 +311,31 @@
     blocks = small(
         merge_kernel,
         place,
-        (near(a_own), near(b_own), near(other)),
-        pltpu.HBM((planes, lead, 2 * quarter), F32),
+        (a_own, b_own, other),
+        [(lead, 2 * quarter)] * planes,
+        [pltpu.VMEM((planes, lead, quarter), F32)],
         flops(lead, lead, half + lead // cores),
     )
-    blocks = exchanged(blocks, "z")
+    blocks = swapped(blocks)
     b_low = shifted(b_own, "core", 1, (0,))
+    held = pltpu.VMEM((planes, lead, quarter), F32)
     mat_shape = (planes - 2, lead, lead // cores)
-    mats_own = small(pick_kernel, place, (far(blocks),), pltpu.VMEM(mat_shape, F32))
+    (mats_own,) = small(pick_kernel, place, blocks, [mat_shape], [held])
     mats_other = shifted(mats_own, "core", 1)
 
     m_high, m_low = pl.pallas_call(
         weigh_kernel,
-        out_shape=[pltpu.HBM((anc, rows), BF16)] * 2,
+        in_specs=[VMEM] * 3,
+        out_specs=[VMEM] * 2,
+        out_shape=[pltpu.VMEM((anc, rows), BF16)] * 2,
         scratch_shapes=[pltpu.VMEM((anc, touched), BF16)],
         cost_estimate=cost(flops(anc, touched, rows + anc), 1 << 22),
         compiler_params=LIMIT,
         name="weigh",
-    )(anc_rows[None], far(anc_inverse), far(coupling))
+    )(anc_rows[None], anc_inverse, coupling)
 
     step = 2 * width
     steps = columns // step
-    tall = pl.BlockSpec((rows, step), lambda j: (0, j))
-    blocked = pl.BlockSpec((step // width, planes, share, width), lambda j: (j, 0, 0, 0))
-    last = pl.BlockSpec((step // width, planes, share, width), lambda j: (steps, 0, 0, 0))
     leaf = pl.pallas_call(
         leaf_kernel,
         grid=(steps + 1,),
@@ -306,11 +345,10 @@
             whole((rows, rows)),
             whole((rows, lead)),
             pl.BlockSpec((rows, step), lambda j: (0, jnp.minimum(j, steps - 1))),
-            whole(b_low.shape),
-            whole(other.shape),
-        ],
-        out_specs=tall,
-        out_shape=pltpu.HBM((rows, columns + lead), F32),
+        ]
+        + [VMEM] * 2,
+        out_specs=VMEM,
+        out_shape=pltpu.VMEM((rows, columns + lead), F32),
         scratch_shapes=[pltpu.VMEM((rows, rows), BF16)] * 2
         + [pltpu.VMEM((rows, lead), BF16)] * 2
         + [pltpu.VMEM((rows, step), F32)],
@@ -320,72 +358,81 @@
     )(
         place,
         block_sizes,
-        far(leaf_inverse),
-        far(leaf_lower),
-        far(leaf_rhs),
-        far(b_low),
-        far(other),
+        leaf_inverse,
+        leaf_lower,
+        leaf_rhs,
+        *[near(a) for a in (b_low, other)],
     )
 
     ends = small(
         solve_kernel,
         place,
-        (far(blocks), near(mats_own), near(mats_other)),
-        pltpu.HBM((planes, lead, quarter), F32),
+        (*blocks, mats_own, mats_other),
+        [(lead, quarter)] * planes,
+        [held, held],
         flops(lead, lead, 2 * quarter),
     )
-    own = exchanged(ends, "z")
+    arrivals = swapped(ends)
+    (own,) = small(gather_kernel, place, arrivals, [(planes, lead, quarter)])
     own_other = shifted(own, "core", 1)
     wide = (columns + lead) // width
     keep, send = pl.pallas_call(
         couple_kernel,
         grid=(steps + 1,),
-        in_specs=[SMEM, whole((anc, rows)), whole((anc, rows)), tall],
-        out_specs=[blocked] * 2,
-        out_shape=[pltpu.HBM((wide, planes, share, width), F32)] * 2,
+        in_specs=[SMEM] + [VMEM] * 3,
+        out_specs=[VMEM] * 2,
+        out_shape=[pltpu.VMEM((wide, planes, share, width), F32)] * 2,
         cost_estimate=cost(flops(anc, rows, columns + lead), 1 << 23),
         compiler_params=LIMIT,
         name="couple",
-    )(place, far(m_high), far(m_low), far(leaf))
+    )(place, *[near(a) for a in (m_high, m_low, leaf)])
     keep_other = shifted(send, "core", 1)
-    ends_spec = whole((planes, lead, quarter))
     update = pl.pallas_call(
         update_kernel,
         grid=(steps,),
-        in_specs=[SMEM, ends_spec, ends_spec, last, last, blocked, blocked],
-        out_specs=blocked,
+        in_specs=[SMEM] + [VMEM] * 4,
+        out_specs=pl.BlockSpec((step // width, planes, share, width), lambda j: (j, 0, 0, 0)),
         out_shape=pltpu.HBM((groups, planes, share, width), F32),
         scratch_shapes=[pltpu.VMEM((planes * share, lead), BF16)] * 2,
         cost_estimate=cost(flops(planes * share, lead, columns), 1 << 22),
         compiler_params=LIMIT,
         name="update",
-    )(place, far(own), near(own_other), *[far(a) for a in (keep, keep_other)] * 2)
+    )(place, *[near(a) for a in (own, own_other, keep, keep_other)])
     update = update.reshape(groups * planes, share, width)
     arrived = exchanged(update, ("x", "yl", "z"))
     sol = pl.pallas_call(
         finish_kernel,
         grid=(steps,),
-        in_specs=[SMEM, ends_spec, ends_spec, pl.BlockSpec((rows, step), lambda j: (0, steps)), tall],
-        out_specs=tall,
+        in_specs=[SMEM] + [VMEM] * 3,
+        out_specs=pl.BlockSpec((rows, step), lambda j: (0, j)),
         out_shape=jax.ShapeDtypeStruct((rows, columns), F32),
         scratch_shapes=[pltpu.VMEM((rows, lead), BF16)] * 2,
         cost_estimate=cost(flops(rows, lead, columns), 1 << 23),
         compiler_params=LIMIT,
         name="finish",
-    )(place, far(own), far(own_other), far(leaf), far(leaf))
+    )(place, near(own), near(own_other), near(leaf))
 
     group = lax.axis_index(("x", "yl"))
     own_rows = lax.dynamic_slice_in_dim(anc_inverse, (z * cores + core) * share, share, 0)
     own_cols = lax.dynamic_slice_in_dim(anc_rhs, group * width, width, 1)
+    right = pl.pallas_call(
+        right_kernel,
+        out_shape=pltpu.HBM((share, width), F32),
+        cost_estimate=cost(flops(share, anc, width), 1 << 20),
+        compiler_params=LIMIT,
+        name="right",
+    )(own_rows, own_cols)
     anc_blocks = pl.pallas_call(
         total_kernel,
-        in_specs=[VMEM] * 3,
+        grid=(planes,),
+        in_specs=[whole((share, width)), pl.BlockSpec((groups, share, width), lambda j: (j, 0, 0))],
         out_specs=VMEM,
         out_shape=pltpu.VMEM((groups, share, width), F32),
-        cost_estimate=cost(flops(share, anc, width), 1 << 21),
+        scratch_shapes=[pltpu.VMEM((share, width), F32)],
+        cost_estimate=cost(1 << 20, 1 << 21),
         compiler_params=LIMIT,
         name="total",
-    )(own_rows, own_cols, near(arrived))
+    )(far(right), far(arrived))
     spread = exchanged(anc_blocks, ("x", "yl"))
     return sol, jnp.moveaxis(spread, 0, 1).reshape(share, columns)
 

time: 118 us -> 110 us (0.932)
  the two profiles are of different devices: /device:TPU:0 before, /device:TPU:1 now
where the time goes in v1:
time: 110 us; the launch traced here: 109 us
  waiting for transfers between devices  38.2 us (35%)
  Pallas kernels  34.3 us (31%)
  starting transfers between devices  28.5 us (26%)
  local copies, waits for them, and re-layouts  6.07 us (6%)
  between operations  1.68 us (2%)
    all_to_all x2, waiting for transfers between devices, exchanged(): return lax.all_to_all(blocks, axes, 0, 0, tiled=True)  19.2 us
    ppermute x11, waiting for transfers between devices, shifted(): return lax.ppermute(array, axis, pairs)  19 us
    ppermute x11, starting transfers between devices, shifted(): return lax.ppermute(array, axis, pairs)  16.4 us
    all_to_all x2, starting transfers between devices, exchanged(): return lax.all_to_all(blocks, axes, 0, 0, tiled=True)  12.2 us
    pallas_call x1, Pallas kernels, whole_body(): pl.pallas_call(leaf_kernel, grid=(steps + 1,), in_specs=[SMEM, SMEM, whol...  7.69 us
    pallas_call x1, Pallas kernels, whole_body(): pl.pallas_call(couple_kernel, grid=(steps + 1,), in_specs=[SMEM] + [VMEM]...  6.11 us
    unnamed x26, local copies, waits for them, and re-layouts  4.24 us
    pallas_call x1, Pallas kernels, whole_body(): pl.pallas_call(finish_kernel, grid=(steps,), in_specs=[SMEM] + [VMEM] * 3...  3.94 us
  transfers between devices with their start and end apart: 13, of which 7 were waited for; matrix products, arithmetic and copies ran while one was open for 1% of the time, Pallas kernels for 11%

profile of v1, /device:TPU:1, one launch (start us, length us, event | category | flops | bytes accessed | tf_op | source)
XLA Modules:
  0.0 108.9 jit_solution(12100804346398118621)
XLA Ops:
  1.5 2.2 %lead.1 = (f32[256,256]{1,0:T(8,128)S(1)}, f32[256,512]{1,0:T(8,128)S(1)}, f32[256,768]{1,0:T(8,128)S(1)}) custom-call(s32[2]{0:T(128)S(1)} %pad_add_fusion.place, s32[1]{0:T(128)S(6)} %copy.13.size, f32[768,768]{1,0:T(8,128)} %inverse.4, f32[768,256]{1,0:T(8,128)} %lower.3, f32[768,1024]{1,0:T(8,128)} %rhs.3), custom_call_target="tpu_custom_call" | custom-call | flops 503316480 | bytes 2097152 | tf_op jit(solution)/shard_map/lead/pallas_call | solution.py:300
  3.8 1.5 %collective-permute-start = (f32[256,768]{1,0:T(8,128)S(1)}, f32[256,768]{1,0:T(8,128)S(1)}, u32[]{:S(2)}, u32[]{:S(2)}) collective-permute-start(f32[256,768]{1,0:T(8,128)S(1)} %get-tuple-element.19), channel_id=1, source_target_pairs={{0,2},{2,0},{1,3},{3,1},{4,6},{6,4},{5,7},{7,5},{8,10},{10,8},{9,1... | collective-permute-start | bytes 2359304 | tf_op jit(solution)/shard_map/ppermute | solution.py:19
  5.2 1.3 %collective-permute-start.9 = (f32[256,512]{1,0:T(8,128)S(1)}, f32[256,512]{1,0:T(8,128)S(1)}, u32[]{:S(2)}, u32[]{:S(2)}) collective-permute-start(f32[256,512]{1,0:T(8,128)S(1)} %get-tuple-element.18.b_own), channel_id=1, source_target_pairs={{0,2},{1,3},{4,6},{5,7},{8,10},{9,11},{12,14},{13,15},{16,18},{17,... | collective-permute-start | bytes 1572872 | tf_op jit(solution)/shard_map/ppermute | solution.py:19
  6.6 3.8 %weigh.1 = (bf16[768,768]{1,0:T(8,128)(2,1)S(1)}, bf16[768,768]{1,0:T(8,128)(2,1)S(1)}) custom-call(s32[1,512]{1,0:T(1,128)S(1)} %bitcast.10, f32[768,768]{1,0:T(8,128)S(1)} %copy-done.10, f32[512,768]{1,0:T(8,128)S(1)} %copy-done.11), custom_call_target="tpu_custom_call" | custom-call | flops 3623878656 | bytes 4194304 | tf_op jit(solution)/shard_map/weigh/pallas_call | solution.py:326
  10.5 7.7 %leaf.1 = f32[768,1280]{1,0:T(8,128)S(1)} custom-call(s32[2]{0:T(128)S(1)} %pad_add_fusion.place, s32[1]{0:T(128)S(6)} %copy.13.size, f32[768,768]{1,0:T(8,128)S(1)} %copy-done.6, f32[768,256]{1,0:T(8,128)S(1)} %copy-done.9, f32[768,1024]{1,0:T(8,128)S(1)} %copy-done.5, f32[256,512]{1,0:T(8,128)S(1)} %collective-permute-done.9.b_first, ...), custom_call_target="tpu_custom_call" | custom-call | flops 3623878656 | bytes 8388608 | tf_op jit(solution)/shard_map/leaf/pallas_call | solution.py:339
  18.2 6.1 %couple.1 = (f32[10,4,96,128]{3,2,1,0:T(8,128)S(1)}, f32[10,4,96,128]{3,2,1,0:T(8,128)S(1)}) custom-call(s32[2]{0:T(128)S(1)} %pad_add_fusion.place, bf16[768,768]{1,0:T(8,128)(2,1)S(1)} %get-tuple-element.28.m_high, bf16[768,768]{1,0:T(8,128)(2,1)S(1)} %get-tuple-element.29.m_low, f32[768,1280]{1,0:T(8,128)S(1)} %leaf.1), custom_call_target="tpu_custom_call" | custom-call | flops 4529848320 | bytes 8388608 | tf_op jit(solution)/shard_map/couple/pallas_call | solution.py:379
  24.3 1.2 %collective-permute-start.10 = (f32[10,4,96,128]{3,2,1,0:T(8,128)S(1)}, f32[10,4,96,128]{3,2,1,0:T(8,128)S(1)}, u32[]{:S(2)}, u32[]{:S(2)}) collective-permute-start(f32[10,4,96,128]{3,2,1,0:T(8,128)S(1)} %get-tuple-element.31), channel_id=1, source_target_pairs={{0,2},{2,0},{1,3},{3,1},{4,6},{6,4},{5,7},{7,5},{8,10},{10,8},{9,1... | collective-permute-start | bytes 5898248 | tf_op jit(solution)/shard_map/ppermute | solution.py:19
  25.5 1.1 %shard_map.95 = (f32[256,256]{1,0:T(8,128)S(1)}, f32[256,256]{1,0:T(8,128)S(1)}, f32[256,256]{1,0:T(8,128)S(1)}, f32[256,256]{1,0:T(8,128)S(1)}) custom-call(s32[2]{0:T(128)S(1)} %pad_add_fusion.place, f32[256,256]{1,0:T(8,128)S(1)} %get-tuple-element.17.a_own, f32[256,512]{1,0:T(8,128)S(1)} %get-tuple-element.18.b_own, ...), custom_call_target="tpu_custom_call" | custom-call | flops 251658240 | bytes 1048576 | tf_op jit(solution)/shard_map/pallas_call | solution.py:69
  26.7 1.8 %collective-permute-start.1 = (f32[256,256]{1,0:T(8,128)S(1)}, f32[256,256]{1,0:T(8,128)S(1)}, u32[]{:S(2)}, u32[]{:S(2)}) collective-permute-start(f32[256,256]{1,0:T(8,128)S(1)} %get-tuple-element.21), channel_id=1, source_target_pairs={{0,4},{4,8},{8,12},{12,0},{1,5},{5,9},{9,13},{13,1},{2,6},{6,10},{... | collective-permute-start | bytes 786440 | tf_op jit(solution)/shard_map/ppermute | solution.py:19
  28.5 3.3 %collective-permute-start.2 = (f32[256,256]{1,0:T(8,128)S(1)}, f32[256,256]{1,0:T(8,128)S(1)}, u32[]{:S(2)}, u32[]{:S(2)}) collective-permute-start(f32[256,256]{1,0:T(8,128)S(1)} %get-tuple-element.22), channel_id=1, source_target_pairs={{0,8},{4,12},{8,0},{12,4},{1,9},{5,13},{9,1},{13,5},{2,10},{6,14},... | collective-permute-start | bytes 786440 | tf_op jit(solution)/shard_map/ppermute | solution.py:19
  32.5 4.8 %collective-permute-done.1.r1 = f32[256,256]{1,0:T(8,128)S(1)} collective-permute-done((f32[256,256]{1,0:T(8,128)S(1)}, f32[256,256]{1,0:T(8,128)S(1)}, u32[]{:S(2)}, u32[]{:S(2)}) %collective-permute-start.1) | collective-permute-done | bytes 262176 | tf_op jit(solution)/shard_map/ppermute | solution.py:19
  37.3 6.5 %collective-permute-done.2.r2 = f32[256,256]{1,0:T(8,128)S(1)} collective-permute-done((f32[256,256]{1,0:T(8,128)S(1)}, f32[256,256]{1,0:T(8,128)S(1)}, u32[]{:S(2)}, u32[]{:S(2)}) %collective-permute-start.2) | collective-permute-done | bytes 262176 | tf_op jit(solution)/shard_map/ppermute | solution.py:19
  44.4 1.0 collective-permute-start.4
  45.3 1.2 %collective-permute-done.4.m_other = f32[2,256,128]{2,1,0:T(8,128)S(1)} collective-permute-done((f32[2,256,128]{2,1,0:T(8,128)S(1)}, f32[2,256,128]{2,1,0:T(8,128)S(1)}, u32[]{:S(2)}, u32[]{:S(2)}) %collective-permute-start.4) | collective-permute-done | bytes 262176 | tf_op jit(solution)/shard_map/ppermute | solution.py:19
  46.5 1.2 %shard_map.97 = (f32[256,128]{1,0:T(8,128)S(1)}, f32[256,128]{1,0:T(8,128)S(1)}, f32[256,128]{1,0:T(8,128)S(1)}, f32[256,128]{1,0:T(8,128)S(1)}) custom-call(s32[2]{0:T(128)S(1)} %pad_add_fusion.place, f32[256,256]{1,0:T(8,128)S(1)} %get-tuple-element.20.r0, f32[256,256]{1,0:T(8,128)S(1)} %collective-permute-done.1.r1, ...), custom_call_target="tpu_custom_call" | custom-call | flops 100663296 | bytes 1048576 | tf_op jit(solution)/shard_map/pallas_call | solution.py:69
  47.7 1.0 collective-permute-start.5
  48.7 2.1 %collective-permute-start.6 = (f32[256,128]{1,0:T(8,128)S(1)}, f32[256,128]{1,0:T(8,128)S(1)}, u32[]{:S(2)}, u32[]{:S(2)}) collective-permute-start(f32[256,128]{1,0:T(8,128)S(1)} %get-tuple-element.26), channel_id=1, source_target_pairs={{0,8},{4,12},{8,0},{12,4},{1,9},{5,13},{9,1},{13,5},{2,10},{6,14},... | collective-permute-start | bytes 393224 | tf_op jit(solution)/shard_map/ppermute | solution.py:19
  50.8 1.0 collective-permute-start.7
  51.8 1.9 %collective-permute-done.5.t1 = f32[256,128]{1,0:T(8,128)S(1)} collective-permute-done((f32[256,128]{1,0:T(8,128)S(1)}, f32[256,128]{1,0:T(8,128)S(1)}, u32[]{:S(2)}, u32[]{:S(2)}) %collective-permute-start.5) | collective-permute-done | bytes 131104 | tf_op jit(solution)/shard_map/ppermute | solution.py:19
  53.6 3.2 %collective-permute-done.6.t2 = f32[256,128]{1,0:T(8,128)S(1)} collective-permute-done((f32[256,128]{1,0:T(8,128)S(1)}, f32[256,128]{1,0:T(8,128)S(1)}, u32[]{:S(2)}, u32[]{:S(2)}) %collective-permute-start.6) | collective-permute-done | bytes 131104 | tf_op jit(solution)/shard_map/ppermute | solution.py:19
  57.4 1.5 %collective-permute-start.8 = (f32[4,256,128]{2,1,0:T(8,128)S(1)}, f32[4,256,128]{2,1,0:T(8,128)S(1)}, u32[]{:S(2)}, u32[]{:S(2)}) collective-permute-start(f32[4,256,128]{2,1,0:T(8,128)S(1)} %shard_map.98.own), channel_id=1, source_target_pairs={{0,2},{2,0},{1,3},{3,1},{4,6},{6,4},{5,7},{7,5},{8,10},{10,8},{9,1... | collective-permute-start | bytes 1572872 | tf_op jit(solution)/shard_map/ppermute | solution.py:19
  58.9 1.5 %collective-permute-done.8.other = f32[4,256,128]{2,1,0:T(8,128)S(1)} collective-permute-done((f32[4,256,128]{2,1,0:T(8,128)S(1)}, f32[4,256,128]{2,1,0:T(8,128)S(1)}, u32[]{:S(2)}, u32[]{:S(2)}) %collective-permute-start.8) | collective-permute-done | bytes 524320 | tf_op jit(solution)/shard_map/ppermute | solution.py:19
  60.5 3.1 %update.1 = f32[8,4,96,128]{3,2,1,0:T(8,128)} custom-call(s32[2]{0:T(128)S(1)} %pad_add_fusion.place, f32[4,256,128]{2,1,0:T(8,128)S(1)} %shard_map.98.own, f32[4,256,128]{2,1,0:T(8,128)S(1)} %collective-permute-done.8.other, f32[10,4,96,128]{3,2,1,0:T(8,128)S(1)} %get-tuple-element.30.keep, f32[10,4,96,128]{3,2,1,0:T(8,128)S(1)} %collective-permute-done.10.arrived), custom_call_target="tpu_custom_call" | custom-call | flops 603979776 | bytes 4194304 | tf_op jit(solution)/shard_map/update/pallas_call | solution.py:390
  63.6 7.6 %all-to-all-start = ((f32[32,96,128]{2,1,0:T(8,128)}), f32[32,96,128]{2,1,0:T(8,128)}, u32[]{:S(2)}, u32[]{:S(2)}) async-start(f32[32,96,128]{2,1,0:T(8,128)} %bitcast.11), calls=%async_computation | async-start | bytes 3145728 | tf_op jit(solution)/shard_map/all_to_all | solution.py:23
  71.3 1.0 constant_dynamic-slice_fusion.1.rows
  73.3 19.2 %all-to-all-done.arrived = f32[32,96,128]{2,1,0:T(8,128)} async-done(((f32[32,96,128]{2,1,0:T(8,128)}), f32[32,96,128]{2,1,0:T(8,128)}, u32[]{:S(2)}, u32[]{:S(2)}) %all-to-all-start) | async-done | bytes 1572896 | tf_op jit(solution)/shard_map/all_to_all | solution.py:23
  92.4 3.0 %total.1 = f32[8,96,128]{2,1,0:T(8,128)} custom-call(f32[96,128]{1,0:T(8,128)} %right.1, f32[32,96,128]{2,1,0:T(8,128)} %all-to-all-done.arrived), custom_call_target="tpu_custom_call" | custom-call | flops 1048576 | bytes 2097152 | tf_op jit(solution)/shard_map/total/pallas_call | solution.py:425
  95.4 4.5 %all-to-all-start.1 = ((f32[8,96,128]{2,1,0:T(8,128)}), f32[8,96,128]{2,1,0:T(8,128)S(1)}, u32[]{:S(2)}, u32[]{:S(2)}) async-start(f32[8,96,128]{2,1,0:T(8,128)} %total.1), calls=%async_computation.1 | async-start | bytes 786432 | tf_op jit(solution)/shard_map/all_to_all | solution.py:23
  99.9 1.0 copy-done.2
  101.0 2.1 %copy-done.4 = f32[768,1280]{1,0:T(8,128)S(1)} copy-done((f32[768,1280]{1,0:T(8,128)S(1)}, f32[768,1280]{1,0:T(8,128)}, u32[]{:S(2)}) %copy-start.4) | copy-done | bytes 3932184
  103.1 1.0 copy-done.8
  104.1 3.9 %finish.1 = f32[768,1024]{1,0:T(8,128)} custom-call(s32[2]{0:T(128)S(1)} %pad_add_fusion.place, f32[4,256,128]{2,1,0:T(8,128)S(1)} %copy-done.2, f32[4,256,128]{2,1,0:T(8,128)S(1)} %copy-done.8, f32[768,1280]{1,0:T(8,128)S(1)} %copy-done.4), custom_call_target="tpu_custom_call" | custom-call | flops 1207959552 | bytes 8388608 | tf_op jit(solution)/shard_map/finish/pallas_call | solution.py:403
  (36 shorter events, 3.8 us)
Async XLA Ops:
  0.6 71.7 %copy-start = (f32[768,1024]{1,0:T(8,128)S(1)}, f32[768,1024]{1,0:T(8,128)}, u32[]{:S(2)}) copy-start(f32[768,1024]{1,0:T(8,128)} %param.14) | copy-start | bytes 9437188
  1.5 5.0 %copy-start.10 = (f32[768,768]{1,0:T(8,128)S(1)}, f32[768,768]{1,0:T(8,128)}, u32[]{:S(2)}) copy-start(f32[768,768]{1,0:T(8,128)} %inverse.5) | copy-start | bytes 7077892
  1.5 5.0 %copy-start.11 = (f32[512,768]{1,0:T(8,128)S(1)}, f32[512,768]{1,0:T(8,128)}, u32[]{:S(2)}) copy-start(f32[512,768]{1,0:T(8,128)} %coupling.1) | copy-start | bytes 4718596
  1.5 5.0 %copy-start.12 = (s32[512]{0:T(512)S(1)}, s32[512]{0:T(512)}, u32[]{:S(2)}) copy-start(s32[512]{0:T(512)} %param.13) | copy-start | bytes 6148
  3.8 6.6 %collective-permute-start = (f32[256,768]{1,0:T(8,128)S(1)}, f32[256,768]{1,0:T(8,128)S(1)}, u32[]{:S(2)}, u32[]{:S(2)}) collective-permute-start(f32[256,768]{1,0:T(8,128)S(1)} %get-tuple-element.19), channel_id=1, source_target_pairs={{0,2},{2,0},{1,3},{3,1},{4,6},{6,4},{5,7},{7,5},{8,10},{10,8},{9,1... | collective-permute-start | bytes 2359304 | tf_op jit(solution)/shard_map/ppermute | solution.py:19
  5.2 5.2 %collective-permute-start.9 = (f32[256,512]{1,0:T(8,128)S(1)}, f32[256,512]{1,0:T(8,128)S(1)}, u32[]{:S(2)}, u32[]{:S(2)}) collective-permute-start(f32[256,512]{1,0:T(8,128)S(1)} %get-tuple-element.18.b_own), channel_id=1, source_target_pairs={{0,2},{1,3},{4,6},{5,7},{8,10},{9,11},{12,14},{13,15},{16,18},{17,... | collective-permute-start | bytes 1572872 | tf_op jit(solution)/shard_map/ppermute | solution.py:19
  6.5 3.9 %copy-start.5 = (f32[768,1024]{1,0:T(8,128)S(1)}, f32[768,1024]{1,0:T(8,128)}, u32[]{:S(2)}) copy-start(f32[768,1024]{1,0:T(8,128)} %rhs.3) | copy-start | bytes 9437188
  6.6 3.9 %copy-start.6 = (f32[768,768]{1,0:T(8,128)S(1)}, f32[768,768]{1,0:T(8,128)}, u32[]{:S(2)}) copy-start(f32[768,768]{1,0:T(8,128)} %inverse.4) | copy-start | bytes 7077892
  6.6 3.9 %copy-start.9 = (f32[768,256]{1,0:T(8,128)S(1)}, f32[768,256]{1,0:T(8,128)}, u32[]{:S(2)}) copy-start(f32[768,256]{1,0:T(8,128)} %lower.3) | copy-start | bytes 2359300
  18.2 6.1 %copy-start.3 = (f32[768,1280]{1,0:T(8,128)}, f32[768,1280]{1,0:T(8,128)S(1)}, u32[]{:S(2)}) copy-start(f32[768,1280]{1,0:T(8,128)S(1)} %leaf.1) | copy-start | bytes 11796484
  24.3 36.2 %collective-permute-start.10 = (f32[10,4,96,128]{3,2,1,0:T(8,128)S(1)}, f32[10,4,96,128]{3,2,1,0:T(8,128)S(1)}, u32[]{:S(2)}, u32[]{:S(2)}) collective-permute-start(f32[10,4,96,128]{3,2,1,0:T(8,128)S(1)} %get-tuple-element.31), channel_id=1, source_target_pairs={{0,2},{2,0},{1,3},{3,1},{4,6},{6,4},{5,7},{7,5},{8,10},{10,8},{9,1... | collective-permute-start | bytes 5898248 | tf_op jit(solution)/shard_map/ppermute | solution.py:19
  26.7 10.6 %collective-permute-start.1 = (f32[256,256]{1,0:T(8,128)S(1)}, f32[256,256]{1,0:T(8,128)S(1)}, u32[]{:S(2)}, u32[]{:S(2)}) collective-permute-start(f32[256,256]{1,0:T(8,128)S(1)} %get-tuple-element.21), channel_id=1, source_target_pairs={{0,4},{4,8},{8,12},{12,0},{1,5},{5,9},{9,13},{13,1},{2,6},{6,10},{... | collective-permute-start | bytes 786440 | tf_op jit(solution)/shard_map/ppermute | solution.py:19
  28.5 15.3 %collective-permute-start.2 = (f32[256,256]{1,0:T(8,128)S(1)}, f32[256,256]{1,0:T(8,128)S(1)}, u32[]{:S(2)}, u32[]{:S(2)}) collective-permute-start(f32[256,256]{1,0:T(8,128)S(1)} %get-tuple-element.22), channel_id=1, source_target_pairs={{0,8},{4,12},{8,0},{12,4},{1,9},{5,13},{9,1},{13,5},{2,10},{6,14},... | collective-permute-start | bytes 786440 | tf_op jit(solution)/shard_map/ppermute | solution.py:19
  31.8 12.0 %collective-permute-start.3 = (f32[256,256]{1,0:T(8,128)S(1)}, f32[256,256]{1,0:T(8,128)S(1)}, u32[]{:S(2)}, u32[]{:S(2)}) collective-permute-start(f32[256,256]{1,0:T(8,128)S(1)} %get-tuple-element.23), channel_id=1, source_target_pairs={{0,12},{4,0},{8,4},{12,8},{1,13},{5,1},{9,5},{13,9},{2,14},{6,2},{... | collective-permute-start | bytes 786440 | tf_op jit(solution)/shard_map/ppermute | solution.py:19
  44.4 2.1 %collective-permute-start.4 = (f32[2,256,128]{2,1,0:T(8,128)S(1)}, f32[2,256,128]{2,1,0:T(8,128)S(1)}, u32[]{:S(2)}, u32[]{:S(2)}) collective-permute-start(f32[2,256,128]{2,1,0:T(8,128)S(1)} %shard_map.96.m_own), channel_id=1, source_target_pairs={{0,2},{2,0},{1,3},{3,1},{4,6},{6,4},{5,7},{7,5},{8,10},{10,8},{9,1... | collective-permute-start | bytes 786440 | tf_op jit(solution)/shard_map/ppermute | solution.py:19
  47.7 6.0 %collective-permute-start.5 = (f32[256,128]{1,0:T(8,128)S(1)}, f32[256,128]{1,0:T(8,128)S(1)}, u32[]{:S(2)}, u32[]{:S(2)}) collective-permute-start(f32[256,128]{1,0:T(8,128)S(1)} %get-tuple-element.25), channel_id=1, source_target_pairs={{0,4},{4,8},{8,12},{12,0},{1,5},{5,9},{9,13},{13,1},{2,6},{6,10},{... | collective-permute-start | bytes 393224 | tf_op jit(solution)/shard_map/ppermute | solution.py:19
  48.7 8.1 %collective-permute-start.6 = (f32[256,128]{1,0:T(8,128)S(1)}, f32[256,128]{1,0:T(8,128)S(1)}, u32[]{:S(2)}, u32[]{:S(2)}) collective-permute-start(f32[256,128]{1,0:T(8,128)S(1)} %get-tuple-element.26), channel_id=1, source_target_pairs={{0,8},{4,12},{8,0},{12,4},{1,9},{5,13},{9,1},{13,5},{2,10},{6,14},... | collective-permute-start | bytes 393224 | tf_op jit(solution)/shard_map/ppermute | solution.py:19
  50.8 6.0 %collective-permute-start.7 = (f32[256,128]{1,0:T(8,128)S(1)}, f32[256,128]{1,0:T(8,128)S(1)}, u32[]{:S(2)}, u32[]{:S(2)}) collective-permute-start(f32[256,128]{1,0:T(8,128)S(1)} %get-tuple-element.27), channel_id=1, source_target_pairs={{0,12},{4,0},{8,4},{12,8},{1,13},{5,1},{9,5},{13,9},{2,14},{6,2},{... | collective-permute-start | bytes 393224 | tf_op jit(solution)/shard_map/ppermute | solution.py:19
  57.4 6.2 %copy-start.1 = (f32[4,256,128]{2,1,0:T(8,128)}, f32[4,256,128]{2,1,0:T(8,128)S(1)}, u32[]{:S(2)}) copy-start(f32[4,256,128]{2,1,0:T(8,128)S(1)} %shard_map.98.own) | copy-start | bytes 1572868
  57.4 3.0 %collective-permute-start.8 = (f32[4,256,128]{2,1,0:T(8,128)S(1)}, f32[4,256,128]{2,1,0:T(8,128)S(1)}, u32[]{:S(2)}, u32[]{:S(2)}) collective-permute-start(f32[4,256,128]{2,1,0:T(8,128)S(1)} %shard_map.98.own), channel_id=1, source_target_pairs={{0,2},{2,0},{1,3},{3,1},{4,6},{6,4},{5,7},{7,5},{8,10},{10,8},{9,1... | collective-permute-start | bytes 1572872 | tf_op jit(solution)/shard_map/ppermute | solution.py:19
  60.5 3.2 %copy-start.7 = (f32[4,256,128]{2,1,0:T(8,128)}, f32[4,256,128]{2,1,0:T(8,128)S(1)}, u32[]{:S(2)}) copy-start(f32[4,256,128]{2,1,0:T(8,128)S(1)} %collective-permute-done.8.other) | copy-start | bytes 1572868
  63.6 28.8 %all-to-all-start = ((f32[32,96,128]{2,1,0:T(8,128)}), f32[32,96,128]{2,1,0:T(8,128)}, u32[]{:S(2)}, u32[]{:S(2)}) async-start(f32[32,96,128]{2,1,0:T(8,128)} %bitcast.11), calls=%async_computation | async-start | bytes 3145728 | tf_op jit(solution)/shard_map/all_to_all | solution.py:23
  95.4 12.7 %all-to-all-start.1 = ((f32[8,96,128]{2,1,0:T(8,128)}), f32[8,96,128]{2,1,0:T(8,128)S(1)}, u32[]{:S(2)}, u32[]{:S(2)}) async-start(f32[8,96,128]{2,1,0:T(8,128)} %total.1), calls=%async_computation.1 | async-start | bytes 786432 | tf_op jit(solution)/shard_map/all_to_all | solution.py:23
  99.9 1.0 copy-start.2
  101.0 2.1 %copy-start.4 = (f32[768,1280]{1,0:T(8,128)S(1)}, f32[768,1280]{1,0:T(8,128)}, u32[]{:S(2)}) copy-start(f32[768,1280]{1,0:T(8,128)} %copy-done.3) | copy-start | bytes 11796484
  103.1 1.0 copy-start.8

commit v2 on v1

--- a/solution.py
+++ b/solution.py
@@ -1,3 +1,5 @@
+import functools
+
 import jax
 import jax.numpy as jnp
 from jax import lax
@@ -98,46 +100,29 @@
     a_high = halves(jnp.where(low, other[:, :lead], a_own[...]))
     b_low = jnp.where(low, b_own[...], other[:, lead:])
     b_high = jnp.where(low, other[:, lead:], b_own[...])
-    planes, tall, width = quarters.shape
-    half = tall // 2
-    rows = tuple(jnp.where(low, part[:half], part[half:]) for part in a_high)
-    mat = dot3(rows, halves(a_low))
+    planes, _, width = quarters.shape
+    mat = dot3(a_high, halves(a_low))
     merged = b_high - dot3(a_high, halves(b_low))
     for i in range(planes):
         quarters[i] = merged[:, i * width : (i + 1) * width]
     for s, out in enumerate((o0, o1, o2, o3)):
         out[:, :width] = quarters[lax.rem(z + s, planes)]
-        out[:half, width:] = mat[:, :width]
-        out[half:, width:] = mat[:, width:]
-
-
-def pick_kernel(place, r0, r1, r2, r3, out, mats):
-    planes, _, width = mats.shape
+        out[:, width:] = mat
+
+
+def solve_kernel(place, r0, r1, r2, r3, o0, o1, o2, o3, blocks, mats, ends):
+    z = place[0]
+    planes, _, width = ends.shape
     for s, r in enumerate((r0, r1, r2, r3)):
-        mats[lax.rem(place[0] + planes - s, planes)] = r[:, width:]
-    for i in range(out.shape[0]):
-        out[i] = mats[i + 1]
-
-
-def solve_kernel(place, r0, r1, r2, r3, m_own, m_other, o0, o1, o2, o3, blocks, ends):
-    z, low = place[0], place[1] == 0
-    planes, _, width = ends.shape
-    half = m_own.shape[1] // 2
-    for s, r in enumerate((r0, r1, r2, r3)):
-        blocks[lax.rem(z + planes - s, planes)] = r[:, :width]
+        at = lax.rem(z + planes - s, planes)
+        blocks[at] = r[:, :width]
+        mats[at] = r[:, width:]
     ends[0] = jnp.zeros(ends.shape[1:], F32)
     carried = blocks[0]
     ends[1] = carried
     for i in range(1, planes - 1):
-        right = halves(carried)
-        for part in range(2):
-            mine = low if part == 0 else jnp.logical_not(low)
-            mat = jnp.where(mine, m_own[i - 1], m_other[i - 1])
-            rows = slice(part * half, (part + 1) * half)
-            moved = dot3(halves(mat[:half]), tuple(r[:width] for r in right))
-            moved += dot3(halves(mat[half:]), tuple(r[width:] for r in right))
-            ends[i + 1, rows] = blocks[i, rows] + moved
-        carried = ends[i + 1]
+        carried = blocks[i] + dot3(halves(mats[i]), halves(carried))
+        ends[i + 1] = carried
     for s, out in enumerate((o0, o1, o2, o3)):
         out[...] = ends[lax.rem(z + s, planes)]
 
@@ -205,13 +190,13 @@
         )
 
 
-def couple_kernel(place, m_high, m_low, leaf, keep, send):
+def couple_kernel(first, place, m_high, m_low, leaf, keep, send):
     low = place[1] == 0
     step = pl.program_id(0)
     planes, share, width = keep.shape[1:]
-    wide = leaf.shape[1] // pl.num_programs(0)
-    value = dot3((m_high[...], m_low[...]), halves(leaf[:, columns_of(step, wide)]))
-    groups = wide // width
+    groups = keep.shape[0] // pl.num_programs(0)
+    cols = columns_of(first + step, groups * width)
+    value = dot3((m_high[...], m_low[...]), halves(leaf[:, cols]))
     for g in range(groups):
         cols = slice(g * width, (g + 1) * width)
         for p in range(planes):
@@ -221,17 +206,14 @@
             send[step * groups + g, p] = jnp.where(low, bottom, top)
 
 
-def entering_chip(place, own, other, step, width):
-    planes, _, quarter = own.shape
-    per = width // quarter
-    half = planes // per
-    first = lax.rem(step, half) * per
-    mine = step // half == place[1]
-    parts = [jnp.where(mine, own[first + i], other[first + i]) for i in range(per)]
+def entering_chip(own, other, mine, first, width):
+    quarter = own.shape[2]
+    parts = [jnp.where(mine, own[first + i], other[first + i]) for i in range(width // quarter)]
     return halves(jnp.concatenate(parts, axis=1))
 
 
-def update_kernel(place, own, other, keep, arrived, out, nh, nl):
+def update_kernel(place, source, n_keep, n_other, c_keep, c_other, *rest):
+    out, nh, nl = rest[-3:]
     groups, planes, share, width = out.shape
     tall, step, steps = planes * share, pl.program_id(0), pl.num_programs(0)
 
@@ -239,25 +221,29 @@
     def _():
         for g in range(groups):
             cols = slice(g * width, (g + 1) * width)
-            n = (keep[steps * groups + g] + arrived[steps * groups + g]).reshape(tall, width)
-            nh[:, cols], nl[:, cols] = halves(n)
-
-    carried = entering_chip(place, own, other, step, groups * width)
-    moved = dot3((nh[...], nl[...]), carried)
+            nh[:, cols], nl[:, cols] = halves((n_keep[g] + n_other[g]).reshape(tall, width))
+
+    own = len(rest) == 3
+    half = place[1] if own else 1 - place[1]
+    parts = [source[step * groups + i] for i in range(groups)]
+    moved = dot3((nh[...], nl[...]), halves(jnp.concatenate(parts, axis=1)))
     for g in range(groups):
-        c = (keep[step * groups + g] + arrived[step * groups + g]).reshape(tall, width)
+        at = (half * steps + step) * groups + g
+        c = (c_keep[at] + c_other[at]).reshape(tall, width)
         out[g] = (c - moved[:, g * width : (g + 1) * width]).reshape(planes, share, width)
 
 
 def finish_kernel(place, own, other, leaf, sol, hh, hl):
-    step = pl.program_id(0)
+    step, steps = pl.program_id(0), pl.num_programs(0)
     width = sol.shape[1]
 
     @pl.when(step == 0)
     def _():
-        hh[...], hl[...] = halves(leaf[:, pl.num_programs(0) * width :])
-
-    carried = entering_chip(place, own, other, step, width)
+        hh[...], hl[...] = halves(leaf[:, steps * width :])
+
+    mine = step // (steps // 2) == place[1]
+    first = lax.rem(step, steps // 2) * (width // own.shape[2])
+    carried = entering_chip(own, other, mine, first, width)
     sol[...] = leaf[:, columns_of(step, width)] - dot3((hh[...], hl[...]), carried)
 
 
@@ -265,24 +251,30 @@
     out[...] = dot3(halves(rows[...]), halves(cols[...]))
 
 
-def total_kernel(right, arrived, out, total):
-    step = pl.program_id(0)
-    part = arrived[0]
-    for i in range(1, arrived.shape[0]):
-        part = part + arrived[i]
-
-    @pl.when(step == 0)
-    def _():
-        total[...] = right[...] - part
-
-    @pl.when(step > 0)
-    def _():
-        total[...] = total[...] - part
-
-    @pl.when(step == pl.num_programs(0) - 1)
-    def _():
-        for g in range(out.shape[0]):
-            out[g] = total[...]
+def total_kernel(right, arrived, out, buffer, sems):
+    chunks = buffer.shape[0]
+    size = buffer.shape[1]
+    copies = [
+        pltpu.make_async_copy(arrived.at[pl.ds(i * size, size)], buffer.at[i], sems.at[i])
+        for i in range(chunks)
+    ]
+    for copy in copies:
+        copy.start()
+    total = right[...]
+    for i, copy in enumerate(copies):
+        copy.wait()
+        for j in range(size):
+            total = total - buffer[i, j]
+    for g in range(out.shape[0]):
+        out[g] = total
+
+
+def lay_kernel(place, spread, out):
+    groups, _, width = spread.shape
+    low = place[1] == 0
+    for g in range(groups):
+        other = (g + groups // 2) % groups
+        out[:, g * width : (g + 1) * width] = jnp.where(low, spread[g], spread[other])
 
 
 def whole_body(leaf_rhs, block_sizes, leaf_lower, leaf_inverse, coupling, anc_rows, anc_rhs, anc_inverse):
@@ -308,21 +300,17 @@
         name="lead",
     )(place, block_sizes, far(leaf_inverse), far(leaf_lower), far(leaf_rhs))
     other = shifted(send, "core", 1)
+    held = pltpu.VMEM((planes, lead, quarter), F32)
     blocks = small(
         merge_kernel,
         place,
         (a_own, b_own, other),
-        [(lead, 2 * quarter)] * planes,
-        [pltpu.VMEM((planes, lead, quarter), F32)],
-        flops(lead, lead, half + lead // cores),
+        [(lead, quarter + lead)] * planes,
+        [held],
+        flops(lead, lead, half + lead),
     )
     blocks = swapped(blocks)
     b_low = shifted(b_own, "core", 1, (0,))
-    held = pltpu.VMEM((planes, lead, quarter), F32)
-    mat_shape = (planes - 2, lead, lead // cores)
-    (mats_own,) = small(pick_kernel, place, blocks, [mat_shape], [held])
-    mats_other = shifted(mats_own, "core", 1)
-
     m_high, m_low = pl.pallas_call(
         weigh_kernel,
         in_specs=[VMEM] * 3,
@@ -364,40 +352,52 @@
         *[near(a) for a in (b_low, other)],
     )
 
+    def couple(first, count):
+        return pl.pallas_call(
+            functools.partial(couple_kernel, first),
+            grid=(count,),
+            in_specs=[SMEM] + [VMEM] * 3,
+            out_specs=[VMEM] * 2,
+            out_shape=[pltpu.VMEM((count * step // width, planes, share, width), F32)] * 2,
+            cost_estimate=cost(flops(anc, rows, count * step), 1 << 23),
+            compiler_params=LIMIT,
+        )(place, *[near(a) for a in (m_high, m_low, leaf)])
+
+    n_keep, n_send = couple(steps, 1)
+    n_other = shifted(n_send, "core", 1)
     ends = small(
         solve_kernel,
         place,
-        (*blocks, mats_own, mats_other),
+        blocks,
         [(lead, quarter)] * planes,
-        [held, held],
+        [held, pltpu.VMEM((planes, lead, lead), F32), held],
         flops(lead, lead, 2 * quarter),
     )
+    c_keep, c_send = couple(0, steps)
+    c_other = shifted(c_send, "core", 1)
     arrivals = swapped(ends)
     (own,) = small(gather_kernel, place, arrivals, [(planes, lead, quarter)])
     own_other = shifted(own, "core", 1)
-    wide = (columns + lead) // width
-    keep, send = pl.pallas_call(
-        couple_kernel,
-        grid=(steps + 1,),
-        in_specs=[SMEM] + [VMEM] * 3,
-        out_specs=[VMEM] * 2,
-        out_shape=[pltpu.VMEM((wide, planes, share, width), F32)] * 2,
-        cost_estimate=cost(flops(anc, rows, columns + lead), 1 << 23),
-        compiler_params=LIMIT,
-        name="couple",
-    )(place, *[near(a) for a in (m_high, m_low, leaf)])
-    keep_other = shifted(send, "core", 1)
-    update = pl.pallas_call(
-        update_kernel,
-        grid=(steps,),
-        in_specs=[SMEM] + [VMEM] * 4,
-        out_specs=pl.BlockSpec((step // width, planes, share, width), lambda j: (j, 0, 0, 0)),
-        out_shape=pltpu.HBM((groups, planes, share, width), F32),
-        scratch_shapes=[pltpu.VMEM((planes * share, lead), BF16)] * 2,
-        cost_estimate=cost(flops(planes * share, lead, columns), 1 << 22),
-        compiler_params=LIMIT,
-        name="update",
-    )(place, *[near(a) for a in (own, own_other, keep, keep_other)])
+
+    def updated(source, ahead):
+        sums = (n_keep, n_other, c_keep, c_other)
+        first = len(ahead) * steps // 2
+        return pl.pallas_call(
+            update_kernel,
+            grid=(steps // 2,),
+            in_specs=[SMEM] + [VMEM] * 5 + [pl.BlockSpec(memory_space=pl.ANY)] * len(ahead),
+            out_specs=pl.BlockSpec(
+                (step // width, planes, share, width), lambda j: (first + j, 0, 0, 0)
+            ),
+            out_shape=pltpu.HBM((groups, planes, share, width), F32),
+            input_output_aliases={6: 0} if ahead else {},
+            scratch_shapes=[pltpu.VMEM((planes * share, lead), BF16)] * 2,
+            cost_estimate=cost(flops(planes * share, lead, half), 1 << 22),
+            compiler_params=LIMIT,
+        )(place, near(source), *[near(a) for a in sums], *ahead)
+
+    update = updated(own, ())
+    update = updated(own_other, (update,))
     update = update.reshape(groups * planes, share, width)
     arrived = exchanged(update, ("x", "yl", "z"))
     sol = pl.pallas_call(
@@ -412,7 +412,7 @@
         name="finish",
     )(place, near(own), near(own_other), near(leaf))
 
-    group = lax.axis_index(("x", "yl"))
+    group = lax.rem(lax.axis_index(("x", "yl")) + core * (groups // 2), groups)
     own_rows = lax.dynamic_slice_in_dim(anc_inverse, (z * cores + core) * share, share, 0)
     own_cols = lax.dynamic_slice_in_dim(anc_rhs, group * width, width, 1)
     right = pl.pallas_call(
@@ -424,17 +424,28 @@
     )(own_rows, own_cols)
     anc_blocks = pl.pallas_call(
         total_kernel,
-        grid=(planes,),
-        in_specs=[whole((share, width)), pl.BlockSpec((groups, share, width), lambda j: (j, 0, 0))],
+        in_specs=[VMEM, pl.BlockSpec(memory_space=pl.ANY)],
         out_specs=VMEM,
         out_shape=pltpu.VMEM((groups, share, width), F32),
-        scratch_shapes=[pltpu.VMEM((share, width), F32)],
+        scratch_shapes=[
+            pltpu.VMEM((planes, groups, share, width), F32),
+            pltpu.SemaphoreType.DMA((planes,)),
+        ],
         cost_estimate=cost(1 << 20, 1 << 21),
         compiler_params=LIMIT,
         name="total",
     )(far(right), far(arrived))
     spread = exchanged(anc_blocks, ("x", "yl"))
-    return sol, jnp.moveaxis(spread, 0, 1).reshape(share, columns)
+    anc = pl.pallas_call(
+        lay_kernel,
+        in_specs=[SMEM, VMEM],
+        out_specs=VMEM,
+        out_shape=jax.ShapeDtypeStruct((share, columns), F32),
+        cost_estimate=cost(1 << 18, 1 << 20),
+        compiler_params=LIMIT,
+        name="lay",
+    )(place, near(spread))
+    return sol, anc
 
 
 def solution(mesh):

time: 110 us -> 115 us (1.045)
  waiting for transfers between devices: 38.2 us -> 43.7 us
  Pallas kernels: 34.3 us -> 35.9 us
  starting transfers between devices: 28.5 us -> 27 us
    ppermute x11, waiting for transfers between devices: 19 us -> 24.2 us  [shifted(): return lax.ppermute(array, axis, pairs)]
    pallas_call x3 -> x6, Pallas kernels: 12.3 us -> 14.3 us  [the longest x2 6.61 us: couple(): pl.pallas_call(functools.partial(couple_kernel, first), grid=(count,), in...]
    unnamed x26 -> x28, local copies, waits for them, and re-layouts: 4.24 us -> 4.98 us
    pallas_call x4 -> x3, Pallas kernels: 3.48 us -> 3.05 us  [small(): pl.pallas_call(kernel, in_specs=[SMEM] + [VMEM] * len(arrays), out_specs=...]
  transfers between devices with their start and end apart: 13 -> 13, of which waited for: 7 -> 6; matrix products, arithmetic and copies ran while one was open for 1% -> 1% of each run, Pallas kernels for 11% -> 13%
where the time goes in v2:
time: 115 us; the launch traced here: 114 us
  waiting for transfers between devices  43.7 us (38%)
  Pallas kernels  35.9 us (31%)
  starting transfers between devices  27 us (23%)
  local copies, waits for them, and re-layouts  6.03 us (5%)
  between operations  1.7 us (1%)
    ppermute x11, waiting for transfers between devices, shifted(): return lax.ppermute(array, axis, pairs)  24.2 us
    all_to_all x2, waiting for transfers between devices, exchanged(): return lax.all_to_all(blocks, axes, 0, 0, tiled=True)  19.5 us
    ppermute x11, starting transfers between devices, shifted(): return lax.ppermute(array, axis, pairs)  15.4 us
    all_to_all x2, starting transfers between devices, exchanged(): return lax.all_to_all(blocks, axes, 0, 0, tiled=True)  11.6 us
    pallas_call x1, Pallas kernels, whole_body(): pl.pallas_call(leaf_kernel, grid=(steps + 1,), in_specs=[SMEM, SMEM, whol...  7.67 us
    pallas_call x2, Pallas kernels, couple(): pl.pallas_call(functools.partial(couple_kernel, first), grid=(count,), in...  6.61 us
    unnamed x28, local copies, waits for them, and re-layouts  4.98 us
    pallas_call x2, Pallas kernels, updated(): pl.pallas_call(update_kernel, grid=(steps // 2,), in_specs=[SMEM] + [VMEM...  4.13 us
  transfers between devices with their start and end apart: 13, of which 6 were waited for; matrix products, arithmetic and copies ran while one was open for 1% of the time, Pallas kernels for 13%

profile of v2, /device:TPU:1, one launch (start us, length us, event | category | flops | bytes accessed | tf_op | source)
XLA Modules:
  0.0 114.4 jit_solution(3196825378831868123)
XLA Ops:
  1.5 2.2 %lead.1 = (f32[256,256]{1,0:T(8,128)S(1)}, f32[256,512]{1,0:T(8,128)S(1)}, f32[256,768]{1,0:T(8,128)S(1)}) custom-call(s32[2]{0:T(128)S(1)} %pad_add_fusion.place, s32[1]{0:T(128)S(6)} %copy.12.size, f32[768,768]{1,0:T(8,128)} %inverse.4, f32[768,256]{1,0:T(8,128)} %lower.3, f32[768,1024]{1,0:T(8,128)} %rhs.3), custom_call_target="tpu_custom_call" | custom-call | flops 503316480 | bytes 2097152 | tf_op jit(solution)/shard_map/lead/pallas_call | solution.py:292
  3.8 1.5 %collective-permute-start = (f32[256,768]{1,0:T(8,128)S(1)}, f32[256,768]{1,0:T(8,128)S(1)}, u32[]{:S(2)}, u32[]{:S(2)}) collective-permute-start(f32[256,768]{1,0:T(8,128)S(1)} %get-tuple-element.21), channel_id=1, source_target_pairs={{0,2},{2,0},{1,3},{3,1},{4,6},{6,4},{5,7},{7,5},{8,10},{10,8},{9,1... | collective-permute-start | bytes 2359304 | tf_op jit(solution)/shard_map/ppermute | solution.py:21
  5.2 1.3 %collective-permute-start.8 = (f32[256,512]{1,0:T(8,128)S(1)}, f32[256,512]{1,0:T(8,128)S(1)}, u32[]{:S(2)}, u32[]{:S(2)}) collective-permute-start(f32[256,512]{1,0:T(8,128)S(1)} %get-tuple-element.20.b_own), channel_id=1, source_target_pairs={{0,2},{1,3},{4,6},{5,7},{8,10},{9,11},{12,14},{13,15},{16,18},{17,... | collective-permute-start | bytes 1572872 | tf_op jit(solution)/shard_map/ppermute | solution.py:21
  6.6 3.8 %weigh.1 = (bf16[768,768]{1,0:T(8,128)(2,1)S(1)}, bf16[768,768]{1,0:T(8,128)(2,1)S(1)}) custom-call(s32[1,512]{1,0:T(1,128)S(1)} %bitcast.4, f32[768,768]{1,0:T(8,128)S(1)} %copy-done.11, f32[512,768]{1,0:T(8,128)S(1)} %copy-done.12), custom_call_target="tpu_custom_call" | custom-call | flops 3623878656 | bytes 4194304 | tf_op jit(solution)/shard_map/weigh/pallas_call | solution.py:314
  10.4 7.7 %leaf.1 = f32[768,1280]{1,0:T(8,128)S(1)} custom-call(s32[2]{0:T(128)S(1)} %pad_add_fusion.place, s32[1]{0:T(128)S(6)} %copy.12.size, f32[768,768]{1,0:T(8,128)S(1)} %copy-done.6, f32[768,256]{1,0:T(8,128)S(1)} %copy-done.10, f32[768,1024]{1,0:T(8,128)S(1)} %copy-done.5, f32[256,512]{1,0:T(8,128)S(1)} %collective-permute-done.8.b_first, ...), custom_call_target="tpu_custom_call" | custom-call | flops 3623878656 | bytes 8388608 | tf_op jit(solution)/shard_map/leaf/pallas_call | solution.py:327
  18.1 5.0 %shard_map.99 = (f32[8,4,96,128]{3,2,1,0:T(8,128)S(1)}, f32[8,4,96,128]{3,2,1,0:T(8,128)S(1)}) custom-call(s32[2]{0:T(128)S(1)} %pad_add_fusion.place, bf16[768,768]{1,0:T(8,128)(2,1)S(1)} %get-tuple-element.30.m_high, bf16[768,768]{1,0:T(8,128)(2,1)S(1)} %get-tuple-element.31.m_low, f32[768,1280]{1,0:T(8,128)S(1)} %leaf.1), custom_call_target="tpu_custom_call" | custom-call | flops 3623878656 | bytes 8388608 | tf_op jit(solution)/shard_map/pallas_call | solution.py:356
  23.1 1.2 %collective-permute-start.10 = (f32[8,4,96,128]{3,2,1,0:T(8,128)S(1)}, f32[8,4,96,128]{3,2,1,0:T(8,128)S(1)}, u32[]{:S(2)}, u32[]{:S(2)}) collective-permute-start(f32[8,4,96,128]{3,2,1,0:T(8,128)S(1)} %get-tuple-element.35), channel_id=1, source_target_pairs={{0,2},{2,0},{1,3},{3,1},{4,6},{6,4},{5,7},{7,5},{8,10},{10,8},{9,1... | collective-permute-start | bytes 4718600 | tf_op jit(solution)/shard_map/ppermute | solution.py:21
  24.3 1.2 %shard_map.95 = (f32[256,384]{1,0:T(8,128)S(1)}, f32[256,384]{1,0:T(8,128)S(1)}, f32[256,384]{1,0:T(8,128)S(1)}, f32[256,384]{1,0:T(8,128)S(1)}) custom-call(s32[2]{0:T(128)S(1)} %pad_add_fusion.place, f32[256,256]{1,0:T(8,128)S(1)} %get-tuple-element.19.a_own, f32[256,512]{1,0:T(8,128)S(1)} %get-tuple-element.20.b_own, ...), custom_call_target="tpu_custom_call" | custom-call | flops 301989888 | bytes 1048576 | tf_op jit(solution)/shard_map/pallas_call | solution.py:71
  25.5 1.8 %collective-permute-start.1 = (f32[256,384]{1,0:T(8,128)S(1)}, f32[256,384]{1,0:T(8,128)S(1)}, u32[]{:S(2)}, u32[]{:S(2)}) collective-permute-start(f32[256,384]{1,0:T(8,128)S(1)} %get-tuple-element.23), channel_id=1, source_target_pairs={{0,4},{4,8},{8,12},{12,0},{1,5},{5,9},{9,13},{13,1},{2,6},{6,10},{... | collective-permute-start | bytes 1179656 | tf_op jit(solution)/shard_map/ppermute | solution.py:21
  27.3 3.3 %collective-permute-start.2 = (f32[256,384]{1,0:T(8,128)S(1)}, f32[256,384]{1,0:T(8,128)S(1)}, u32[]{:S(2)}, u32[]{:S(2)}) collective-permute-start(f32[256,384]{1,0:T(8,128)S(1)} %get-tuple-element.24), channel_id=1, source_target_pairs={{0,8},{4,12},{8,0},{12,4},{1,9},{5,13},{9,1},{13,5},{2,10},{6,14},... | collective-permute-start | bytes 1179656 | tf_op jit(solution)/shard_map/ppermute | solution.py:21
  31.4 7.6 %collective-permute-done.1.r1 = f32[256,384]{1,0:T(8,128)S(1)} collective-permute-done((f32[256,384]{1,0:T(8,128)S(1)}, f32[256,384]{1,0:T(8,128)S(1)}, u32[]{:S(2)}, u32[]{:S(2)}) %collective-permute-start.1) | collective-permute-done | bytes 393248 | tf_op jit(solution)/shard_map/ppermute | solution.py:21
  38.9 9.3 %collective-permute-done.2.r2 = f32[256,384]{1,0:T(8,128)S(1)} collective-permute-done((f32[256,384]{1,0:T(8,128)S(1)}, f32[256,384]{1,0:T(8,128)S(1)}, u32[]{:S(2)}, u32[]{:S(2)}) %collective-permute-start.2) | collective-permute-done | bytes 393248 | tf_op jit(solution)/shard_map/ppermute | solution.py:21
  48.3 1.3 %shard_map.96 = (f32[256,128]{1,0:T(8,128)S(1)}, f32[256,128]{1,0:T(8,128)S(1)}, f32[256,128]{1,0:T(8,128)S(1)}, f32[256,128]{1,0:T(8,128)S(1)}) custom-call(s32[2]{0:T(128)S(1)} %pad_add_fusion.place, f32[256,384]{1,0:T(8,128)S(1)} %get-tuple-element.22.r0, f32[256,384]{1,0:T(8,128)S(1)} %collective-permute-done.1.r1, ...), custom_call_target="tpu_custom_call" | custom-call | flops 100663296 | bytes 1048576 | tf_op jit(solution)/shard_map/pallas_call | solution.py:71
  49.6 1.0 collective-permute-start.4
  50.6 2.5 %collective-permute-start.5 = (f32[256,128]{1,0:T(8,128)S(1)}, f32[256,128]{1,0:T(8,128)S(1)}, u32[]{:S(2)}, u32[]{:S(2)}) collective-permute-start(f32[256,128]{1,0:T(8,128)S(1)} %get-tuple-element.28), channel_id=1, source_target_pairs={{0,8},{4,12},{8,0},{12,4},{1,9},{5,13},{9,1},{13,5},{2,10},{6,14},... | collective-permute-start | bytes 393224 | tf_op jit(solution)/shard_map/ppermute | solution.py:21
  53.4 1.6 %collective-permute-done.4.t1 = f32[256,128]{1,0:T(8,128)S(1)} collective-permute-done((f32[256,128]{1,0:T(8,128)S(1)}, f32[256,128]{1,0:T(8,128)S(1)}, u32[]{:S(2)}, u32[]{:S(2)}) %collective-permute-start.4) | collective-permute-done | bytes 131104 | tf_op jit(solution)/shard_map/ppermute | solution.py:21
  55.0 4.0 %collective-permute-done.5.t2 = f32[256,128]{1,0:T(8,128)S(1)} collective-permute-done((f32[256,128]{1,0:T(8,128)S(1)}, f32[256,128]{1,0:T(8,128)S(1)}, u32[]{:S(2)}, u32[]{:S(2)}) %collective-permute-start.5) | collective-permute-done | bytes 131104 | tf_op jit(solution)/shard_map/ppermute | solution.py:21
  59.6 1.4 %collective-permute-start.7 = (f32[4,256,128]{2,1,0:T(8,128)S(1)}, f32[4,256,128]{2,1,0:T(8,128)S(1)}, u32[]{:S(2)}, u32[]{:S(2)}) collective-permute-start(f32[4,256,128]{2,1,0:T(8,128)S(1)} %shard_map.97.own.source), channel_id=1, source_target_pairs={{0,2},{2,0},{1,3},{3,1},{4,6},{6,4},{5,7},{7,5},{8,10},{10,8},{9,1... | collective-permute-start | bytes 1572872 | tf_op jit(solution)/shard_map/ppermute | solution.py:21
  61.0 1.6 %shard_map.98 = (f32[2,4,96,128]{3,2,1,0:T(8,128)S(1)}, f32[2,4,96,128]{3,2,1,0:T(8,128)S(1)}) custom-call(s32[2]{0:T(128)S(1)} %pad_add_fusion.place, bf16[768,768]{1,0:T(8,128)(2,1)S(1)} %get-tuple-element.30.m_high, bf16[768,768]{1,0:T(8,128)(2,1)S(1)} %get-tuple-element.31.m_low, f32[768,1280]{1,0:T(8,128)S(1)} %leaf.1), custom_call_target="tpu_custom_call" | custom-call | flops 905969664 | bytes 8388608 | tf_op jit(solution)/shard_map/pallas_call | solution.py:356
  62.9 1.7 %collective-permute-done.9.n_other = f32[2,4,96,128]{3,2,1,0:T(8,128)S(1)} collective-permute-done((f32[2,4,96,128]{3,2,1,0:T(8,128)S(1)}, f32[2,4,96,128]{3,2,1,0:T(8,128)S(1)}, u32[]{:S(2)}, u32[]{:S(2)}) %collective-permute-start.9) | collective-permute-done | bytes 393248 | tf_op jit(solution)/shard_map/ppermute | solution.py:21
  64.7 2.1 %shard_map.100.rest_0_ = f32[8,4,96,128]{3,2,1,0:T(8,128)} custom-call(s32[2]{0:T(128)S(1)} %pad_add_fusion.place, f32[4,256,128]{2,1,0:T(8,128)S(1)} %shard_map.97.own.source, f32[2,4,96,128]{3,2,1,0:T(8,128)S(1)} %get-tuple-element.32.n_keep, f32[2,4,96,128]{3,2,1,0:T(8,128)S(1)} %collective-permute-done.9.n_other, ...), custom_call_target="tpu_custom_call" | custom-call | flops 301989888 | bytes 4194304 | tf_op jit(solution)/shard_map/pallas_call | solution.py:385
  66.7 2.1 %shard_map.101 = f32[8,4,96,128]{3,2,1,0:T(8,128)} custom-call(s32[2]{0:T(128)S(1)} %pad_add_fusion.place, f32[4,256,128]{2,1,0:T(8,128)S(1)} %collective-permute-done.7.other.source, f32[2,4,96,128]{3,2,1,0:T(8,128)S(1)} %get-tuple-element.32.n_keep, f32[2,4,96,128]{3,2,1,0:T(8,128)S(1)} %collective-permute-done.9.n_other, ...), custom_call_target="tpu_custom_call", output_to_operand_aliasing={{}: (6, {})} | custom-call | flops 301989888 | bytes 4194304 | tf_op jit(solution)/shard_map/pallas_call | solution.py:385
  68.8 7.4 %all-to-all-start = ((f32[32,96,128]{2,1,0:T(8,128)}), f32[32,96,128]{2,1,0:T(8,128)}, u32[]{:S(2)}, u32[]{:S(2)}) async-start(f32[32,96,128]{2,1,0:T(8,128)} %bitcast.5), calls=%async_computation | async-start | bytes 3145728 | tf_op jit(solution)/shard_map/all_to_all | solution.py:25
  76.2 1.0 constant_dynamic-slice_fusion.1.rows
  78.2 19.5 %all-to-all-done.arrived = f32[32,96,128]{2,1,0:T(8,128)} async-done(((f32[32,96,128]{2,1,0:T(8,128)}), f32[32,96,128]{2,1,0:T(8,128)}, u32[]{:S(2)}, u32[]{:S(2)}) %all-to-all-start) | async-done | bytes 1572896 | tf_op jit(solution)/shard_map/all_to_all | solution.py:25
  97.7 2.2 %total.1 = f32[8,96,128]{2,1,0:T(8,128)S(1)} custom-call(f32[96,128]{1,0:T(8,128)} %right.1, f32[32,96,128]{2,1,0:T(8,128)} %all-to-all-done.arrived), custom_call_target="tpu_custom_call" | custom-call | flops 1048576 | bytes 2097152 | tf_op jit(solution)/shard_map/total/pallas_call | solution.py:425
  100.7 4.2 %all-to-all-start.1 = ((f32[8,96,128]{2,1,0:T(8,128)}), f32[8,96,128]{2,1,0:T(8,128)S(1)}, u32[]{:S(2)}, u32[]{:S(2)}) async-start(f32[8,96,128]{2,1,0:T(8,128)} %copy-done.9), calls=%async_computation.1 | async-start | bytes 786432 | tf_op jit(solution)/shard_map/all_to_all | solution.py:25
  104.9 2.1 %copy-done.2 = f32[768,1280]{1,0:T(8,128)S(1)} copy-done((f32[768,1280]{1,0:T(8,128)S(1)}, f32[768,1280]{1,0:T(8,128)}, u32[]{:S(2)}) %copy-start.2) | copy-done | bytes 3932184
  107.0 1.0 copy-done.4
  108.1 1.0 copy-done.8
  109.1 3.9 %finish.1 = f32[768,1024]{1,0:T(8,128)} custom-call(s32[2]{0:T(128)S(1)} %pad_add_fusion.place, f32[4,256,128]{2,1,0:T(8,128)S(1)} %copy-done.4, f32[4,256,128]{2,1,0:T(8,128)S(1)} %copy-done.8, f32[768,1280]{1,0:T(8,128)S(1)} %copy-done.2), custom_call_target="tpu_custom_call" | custom-call | flops 1207959552 | bytes 8388608 | tf_op jit(solution)/shard_map/finish/pallas_call | solution.py:403
  113.0 1.3 %lay.1 = f32[96,1024]{1,0:T(8,128)} custom-call(s32[2]{0:T(128)S(1)} %pad_add_fusion.place, f32[8,96,128]{2,1,0:T(8,128)S(1)} %all-to-all-done.1.spread), custom_call_target="tpu_custom_call" | custom-call | flops 262144 | bytes 1048576 | tf_op jit(solution)/shard_map/lay/pallas_call | solution.py:439
  (39 shorter events, 3.8 us)
Async XLA Ops:
  0.6 76.6 %copy-start = (f32[768,1024]{1,0:T(8,128)S(1)}, f32[768,1024]{1,0:T(8,128)}, u32[]{:S(2)}) copy-start(f32[768,1024]{1,0:T(8,128)} %param.14) | copy-start | bytes 9437188
  1.5 5.0 %copy-start.11 = (f32[768,768]{1,0:T(8,128)S(1)}, f32[768,768]{1,0:T(8,128)}, u32[]{:S(2)}) copy-start(f32[768,768]{1,0:T(8,128)} %inverse.5) | copy-start | bytes 7077892
  1.5 5.0 %copy-start.12 = (f32[512,768]{1,0:T(8,128)S(1)}, f32[512,768]{1,0:T(8,128)}, u32[]{:S(2)}) copy-start(f32[512,768]{1,0:T(8,128)} %coupling.1) | copy-start | bytes 4718596
  1.5 5.0 %copy-start.13 = (s32[512]{0:T(512)S(1)}, s32[512]{0:T(512)}, u32[]{:S(2)}) copy-start(s32[512]{0:T(512)} %param.13) | copy-start | bytes 6148
  3.8 6.6 %collective-permute-start = (f32[256,768]{1,0:T(8,128)S(1)}, f32[256,768]{1,0:T(8,128)S(1)}, u32[]{:S(2)}, u32[]{:S(2)}) collective-permute-start(f32[256,768]{1,0:T(8,128)S(1)} %get-tuple-element.21), channel_id=1, source_target_pairs={{0,2},{2,0},{1,3},{3,1},{4,6},{6,4},{5,7},{7,5},{8,10},{10,8},{9,1... | collective-permute-start | bytes 2359304 | tf_op jit(solution)/shard_map/ppermute | solution.py:21
  5.2 5.2 %collective-permute-start.8 = (f32[256,512]{1,0:T(8,128)S(1)}, f32[256,512]{1,0:T(8,128)S(1)}, u32[]{:S(2)}, u32[]{:S(2)}) collective-permute-start(f32[256,512]{1,0:T(8,128)S(1)} %get-tuple-element.20.b_own), channel_id=1, source_target_pairs={{0,2},{1,3},{4,6},{5,7},{8,10},{9,11},{12,14},{13,15},{16,18},{17,... | collective-permute-start | bytes 1572872 | tf_op jit(solution)/shard_map/ppermute | solution.py:21
  6.5 3.9 %copy-start.5 = (f32[768,1024]{1,0:T(8,128)S(1)}, f32[768,1024]{1,0:T(8,128)}, u32[]{:S(2)}) copy-start(f32[768,1024]{1,0:T(8,128)} %rhs.3) | copy-start | bytes 9437188
  6.6 3.9 %copy-start.6 = (f32[768,768]{1,0:T(8,128)S(1)}, f32[768,768]{1,0:T(8,128)}, u32[]{:S(2)}) copy-start(f32[768,768]{1,0:T(8,128)} %inverse.4) | copy-start | bytes 7077892
  6.6 3.9 %copy-start.10 = (f32[768,256]{1,0:T(8,128)S(1)}, f32[768,256]{1,0:T(8,128)}, u32[]{:S(2)}) copy-start(f32[768,256]{1,0:T(8,128)} %lower.3) | copy-start | bytes 2359300
  18.1 42.9 %copy-start.1 = (f32[768,1280]{1,0:T(8,128)}, f32[768,1280]{1,0:T(8,128)S(1)}, u32[]{:S(2)}) copy-start(f32[768,1280]{1,0:T(8,128)S(1)} %leaf.1) | copy-start | bytes 11796484
  23.1 41.5 %collective-permute-start.10 = (f32[8,4,96,128]{3,2,1,0:T(8,128)S(1)}, f32[8,4,96,128]{3,2,1,0:T(8,128)S(1)}, u32[]{:S(2)}, u32[]{:S(2)}) collective-permute-start(f32[8,4,96,128]{3,2,1,0:T(8,128)S(1)} %get-tuple-element.35), channel_id=1, source_target_pairs={{0,2},{2,0},{1,3},{3,1},{4,6},{6,4},{5,7},{7,5},{8,10},{10,8},{9,1... | collective-permute-start | bytes 4718600 | tf_op jit(solution)/shard_map/ppermute | solution.py:21
  25.5 13.4 %collective-permute-start.1 = (f32[256,384]{1,0:T(8,128)S(1)}, f32[256,384]{1,0:T(8,128)S(1)}, u32[]{:S(2)}, u32[]{:S(2)}) collective-permute-start(f32[256,384]{1,0:T(8,128)S(1)} %get-tuple-element.23), channel_id=1, source_target_pairs={{0,4},{4,8},{8,12},{12,0},{1,5},{5,9},{9,13},{13,1},{2,6},{6,10},{... | collective-permute-start | bytes 1179656 | tf_op jit(solution)/shard_map/ppermute | solution.py:21
  27.3 20.9 %collective-permute-start.2 = (f32[256,384]{1,0:T(8,128)S(1)}, f32[256,384]{1,0:T(8,128)S(1)}, u32[]{:S(2)}, u32[]{:S(2)}) collective-permute-start(f32[256,384]{1,0:T(8,128)S(1)} %get-tuple-element.24), channel_id=1, source_target_pairs={{0,8},{4,12},{8,0},{12,4},{1,9},{5,13},{9,1},{13,5},{2,10},{6,14},... | collective-permute-start | bytes 1179656 | tf_op jit(solution)/shard_map/ppermute | solution.py:21
  30.6 17.6 %collective-permute-start.3 = (f32[256,384]{1,0:T(8,128)S(1)}, f32[256,384]{1,0:T(8,128)S(1)}, u32[]{:S(2)}, u32[]{:S(2)}) collective-permute-start(f32[256,384]{1,0:T(8,128)S(1)} %get-tuple-element.25), channel_id=1, source_target_pairs={{0,12},{4,0},{8,4},{12,8},{1,13},{5,1},{9,5},{13,9},{2,14},{6,2},{... | collective-permute-start | bytes 1179656 | tf_op jit(solution)/shard_map/ppermute | solution.py:21
  49.6 5.5 %collective-permute-start.4 = (f32[256,128]{1,0:T(8,128)S(1)}, f32[256,128]{1,0:T(8,128)S(1)}, u32[]{:S(2)}, u32[]{:S(2)}) collective-permute-start(f32[256,128]{1,0:T(8,128)S(1)} %get-tuple-element.27), channel_id=1, source_target_pairs={{0,4},{4,8},{8,12},{12,0},{1,5},{5,9},{9,13},{13,1},{2,6},{6,10},{... | collective-permute-start | bytes 393224 | tf_op jit(solution)/shard_map/ppermute | solution.py:21
  50.6 8.4 %collective-permute-start.5 = (f32[256,128]{1,0:T(8,128)S(1)}, f32[256,128]{1,0:T(8,128)S(1)}, u32[]{:S(2)}, u32[]{:S(2)}) collective-permute-start(f32[256,128]{1,0:T(8,128)S(1)} %get-tuple-element.28), channel_id=1, source_target_pairs={{0,8},{4,12},{8,0},{12,4},{1,9},{5,13},{9,1},{13,5},{2,10},{6,14},... | collective-permute-start | bytes 393224 | tf_op jit(solution)/shard_map/ppermute | solution.py:21
  53.1 5.9 %collective-permute-start.6 = (f32[256,128]{1,0:T(8,128)S(1)}, f32[256,128]{1,0:T(8,128)S(1)}, u32[]{:S(2)}, u32[]{:S(2)}) collective-permute-start(f32[256,128]{1,0:T(8,128)S(1)} %get-tuple-element.29), channel_id=1, source_target_pairs={{0,12},{4,0},{8,4},{12,8},{1,13},{5,1},{9,5},{13,9},{2,14},{6,2},{... | collective-permute-start | bytes 393224 | tf_op jit(solution)/shard_map/ppermute | solution.py:21
  59.6 5.1 %copy-start.3 = (f32[4,256,128]{2,1,0:T(8,128)}, f32[4,256,128]{2,1,0:T(8,128)S(1)}, u32[]{:S(2)}) copy-start(f32[4,256,128]{2,1,0:T(8,128)S(1)} %shard_map.97.own.source) | copy-start | bytes 1572868
  59.6 7.1 %collective-permute-start.7 = (f32[4,256,128]{2,1,0:T(8,128)S(1)}, f32[4,256,128]{2,1,0:T(8,128)S(1)}, u32[]{:S(2)}, u32[]{:S(2)}) collective-permute-start(f32[4,256,128]{2,1,0:T(8,128)S(1)} %shard_map.97.own.source), channel_id=1, source_target_pairs={{0,2},{2,0},{1,3},{3,1},{4,6},{6,4},{5,7},{7,5},{8,10},{10,8},{9,1... | collective-permute-start | bytes 1572872 | tf_op jit(solution)/shard_map/ppermute | solution.py:21
  62.7 2.0 %collective-permute-start.9 = (f32[2,4,96,128]{3,2,1,0:T(8,128)S(1)}, f32[2,4,96,128]{3,2,1,0:T(8,128)S(1)}, u32[]{:S(2)}, u32[]{:S(2)}) collective-permute-start(f32[2,4,96,128]{3,2,1,0:T(8,128)S(1)} %get-tuple-element.33), channel_id=1, source_target_pairs={{0,2},{2,0},{1,3},{3,1},{4,6},{6,4},{5,7},{7,5},{8,10},{10,8},{9,1... | collective-permute-start | bytes 1179656 | tf_op jit(solution)/shard_map/ppermute | solution.py:21
  66.7 2.1 %copy-start.7 = (f32[4,256,128]{2,1,0:T(8,128)}, f32[4,256,128]{2,1,0:T(8,128)S(1)}, u32[]{:S(2)}) copy-start(f32[4,256,128]{2,1,0:T(8,128)S(1)} %collective-permute-done.7.other.source) | copy-start | bytes 1572868
  68.8 29.0 %all-to-all-start = ((f32[32,96,128]{2,1,0:T(8,128)}), f32[32,96,128]{2,1,0:T(8,128)}, u32[]{:S(2)}, u32[]{:S(2)}) async-start(f32[32,96,128]{2,1,0:T(8,128)} %bitcast.5), calls=%async_computation | async-start | bytes 3145728 | tf_op jit(solution)/shard_map/all_to_all | solution.py:25
  100.0 0.7 copy-start.9
  100.7 12.3 %all-to-all-start.1 = ((f32[8,96,128]{2,1,0:T(8,128)}), f32[8,96,128]{2,1,0:T(8,128)S(1)}, u32[]{:S(2)}, u32[]{:S(2)}) async-start(f32[8,96,128]{2,1,0:T(8,128)} %copy-done.9), calls=%async_computation.1 | async-start | bytes 786432 | tf_op jit(solution)/shard_map/all_to_all | solution.py:25
  104.9 2.1 %copy-start.2 = (f32[768,1280]{1,0:T(8,128)S(1)}, f32[768,1280]{1,0:T(8,128)}, u32[]{:S(2)}) copy-start(f32[768,1280]{1,0:T(8,128)} %copy-done.1) | copy-start | bytes 11796484
  107.0 1.0 copy-start.4
  108.1 1.0 copy-start.8
